TPU v7x, 32 devices: a whole 2x2x4 slice. The times are simulated.
32 devices in a mesh: blk: 8 (over z, core), section: 4 (over y, x).
Axes of the slice: x: 2, y: 2, z: 4, core: 2. Of those that a mesh axis runs over, the one named last changes fastest.
Arguments:
- hidden: bfloat16 [4, 2048, 4096], P('section', 'blk'), parts along dimension 1, may hold values from -6 to 6
- exit_layer: int32 [4096], P('blk'), parts along dimension 0, may hold values from 1 to 2
- lengths: int32 [4096], P('blk'), parts along dimension 0, may hold values from 1 to 16, as said below
- kv_cache: bfloat16 [4, 2048, 16, 256], P('section', 'blk'), parts along dimension 1, may hold values from -256 to 256
- norm_gain: bfloat16 [4, 4096], P('section'), may hold values from 0.5 to 1.5
- w_qkv: bfloat16 [4, 4096, 1280], P('section'), may hold values from -0.0625 to 0.0625
- w_out: bfloat16 [4, 1024, 4096], P('section'), may hold values from -0.1875 to 0.1875
Outputs:
- settled: bfloat16 [4096, 8192], P('blk', 'section'), parts along dimension 0
There are 8 independent parts, one for each index of `blk`. A program takes and returns all parts, laid end to end along the dimension named above; an argument that names none is the same for every part. Nothing has to cross between parts.
Inputs may be any that keep to these rules, and one draw needn't show every extreme that they name: `lengths`: some token has length 16.
All inputs are finite; a program needn't handle non-finite values.
Results may differ from a plain program's by a relative error of at most 0.03.
Values may be sent and summed in bfloat16 or wider, within the bound.
No kernel may reach another device: no remote copies, remote signals or barrier semaphores. Data moves between devices by JAX's collectives and lax.ppermute only.
A program may use at most 64 MiB of HBM per device.

v0:
```python
import math

import jax
import jax.numpy as jnp
from jax import lax
from jax.sharding import PartitionSpec as P

BLOCK = 64
MICRO = 8


EPSILON = 1e-05
NEGATIVE = -1e30


def partner(value, axis, distance):
    return lax.ppermute(value, axis, [(i, i ^ 1 << distance) for i in range(lax.axis_size(axis))])


def shifted(value, axis, steps):
    count = lax.axis_size(axis)
    pairs = [(source, (source + steps) % count) for source in range(count)]
    return lax.ppermute(value, axis, pairs)


def body(hidden, exit_layer, lengths, kv_cache, norm_gain, w_qkv, w_out):
    devices = lax.axis_size("section")
    index = lax.axis_index("section")
    shards = max(2, devices // 4)
    cycle_size = devices // shards
    segment_bits = cycle_size.bit_length() - 1
    shard_bits = shards.bit_length() - 1
    segment_index = index // shards
    shard_index = index % shards
    own_blocks = hidden[0]
    gain_row = norm_gain[0].astype(jnp.float32)
    proj_weight = w_qkv[0]
    out_weight = w_out[0]
    cache_all = kv_cache[0]
    query_width = out_weight.shape[0]
    head_size = (proj_weight.shape[1] - query_width) // 2
    heads = query_width // head_size
    quarter = proj_weight.shape[0]
    total_width = quarter * shards
    group_rows = BLOCK // shards
    rounds = MICRO // cycle_size
    context = cache_all.shape[1]
    positions = jnp.arange(context, dtype=jnp.int32)
    blank_block = jnp.zeros((BLOCK, quarter), jnp.bfloat16)

    def advance(carry, microstep):
        incoming, arriving, records = carry
        micro_index = microstep - segment_index
        in_range = (micro_index >= 0) & (micro_index < MICRO)
        slot = jnp.clip(micro_index, 0, MICRO - 1)
        on_turn = microstep % cycle_size == 0
        local_slot = jnp.minimum(microstep // cycle_size, rounds - 1)
        own_block = lax.dynamic_slice_in_dim(own_blocks, local_slot * BLOCK, BLOCK, 0)
        exit_rows = lax.dynamic_slice_in_dim(exit_layer, slot * BLOCK, BLOCK)
        own_lengths = lax.dynamic_slice_in_dim(
            lengths, slot * BLOCK + shard_index * group_rows, group_rows
        )
        own_cache = lax.dynamic_slice_in_dim(cache_all, slot * group_rows, group_rows, 0)
        first_input = jnp.where(on_turn, own_block, arriving)
        entering = jnp.where(segment_index == 0, first_input, incoming)
        active = exit_rows > segment_index
        gate = in_range & (jnp.sum(active.astype(jnp.int32)) > 0)

        def local_partials():
            widened = entering.astype(jnp.float32)
            scaled = (widened * gain_row).astype(jnp.bfloat16)
            return (
                jnp.dot(scaled, proj_weight, preferred_element_type=jnp.float32),
                jnp.sum(widened * widened, axis=1),
            )

        def no_partials():
            return (
                jnp.zeros((BLOCK, proj_weight.shape[1]), jnp.float32),
                jnp.zeros((BLOCK,), jnp.float32),
            )

        partial_proj, partial_squares = lax.cond(gate, local_partials, no_partials)
        kept = (partial_proj, partial_squares)
        for level in range(shard_bits):
            bit = shard_bits - 1 - level
            upper = index >> bit & 1
            halves = tuple(
                (piece.reshape((2, piece.shape[0] // 2) + piece.shape[1:]) for piece in kept)
            )
            keep = tuple((jnp.where(upper == 1, half[1], half[0]) for half in halves))
            send = tuple((jnp.where(upper == 1, half[0], half[1]) for half in halves))
            received = partner(send, "section", bit)
            kept = tuple((first + second for first, second in zip(keep, received)))
        own_proj, own_squares = kept

        def local_attention():
            fitted = own_proj * lax.rsqrt(own_squares / total_width + EPSILON)[:, None]
            query = (fitted[:, :query_width] * (1.0 / math.sqrt(head_size))).astype(jnp.bfloat16)
            query = query.reshape(group_rows, heads, head_size)
            key_new = fitted[:, query_width : query_width + head_size].astype(jnp.bfloat16)
            value_new = fitted[:, query_width + head_size :].astype(jnp.bfloat16)
            scores = jnp.einsum(
                "rhd,rcd->rhc",
                query,
                own_cache[:, :, :head_size],
                preferred_element_type=jnp.float32,
            )
            own = jnp.einsum("rhd,rd->rh", query, key_new, preferred_element_type=jnp.float32)
            usable = (positions[None, :] < own_lengths[:, None])[:, None, :]
            scores = jnp.where(usable, scores, NEGATIVE)
            row_top = jnp.maximum(jnp.max(scores, axis=-1), own)
            raw = jnp.where(usable, jnp.exp(scores - row_top[:, :, None]), jnp.float32(0.0))
            raw_own = jnp.exp(own - row_top)
            total = jnp.sum(raw, axis=-1) + raw_own
            weights = (raw / total[:, :, None]).astype(jnp.bfloat16)
            own_weight = (raw_own / total).astype(jnp.bfloat16)
            attended = jnp.einsum(
                "rhc,rcd->rhd",
                weights,
                own_cache[:, :, head_size:],
                preferred_element_type=jnp.float32,
            )
            attended = (
                attended
                + own_weight.astype(jnp.float32)[:, :, None]
                * value_new.astype(jnp.float32)[:, None, :]
            )
            return attended.astype(jnp.bfloat16).reshape(group_rows, query_width)

        def no_attention():
            return jnp.zeros((group_rows, query_width), jnp.bfloat16)

        collected = lax.cond(gate, local_attention, no_attention)
        for level in range(shard_bits):
            bit = level
            other = partner(collected, "section", bit)
            upper = index >> bit & 1
            collected = jnp.where(
                upper == 1,
                jnp.concatenate([other, collected], 0),
                jnp.concatenate([collected, other], 0),
            )

        def local_update():
            branch_out = jnp.dot(collected, out_weight, preferred_element_type=jnp.float32)
            updated = (entering.astype(jnp.float32) + branch_out).astype(jnp.bfloat16)
            return jnp.where(active[:, None], updated, entering)

        def keep_state():
            return entering

        outgoing = lax.cond(gate, local_update, keep_state)
        leaving = in_range & (exit_rows == segment_index + 1)
        previous = lax.dynamic_slice_in_dim(records, slot * BLOCK, BLOCK, 0)
        records = lax.dynamic_update_slice_in_dim(
            records, jnp.where(leaving[:, None], outgoing, previous), slot * BLOCK, 0
        )
        relayed = jnp.where(on_turn & (segment_index > 0), own_block, arriving)
        incoming, arriving = shifted((outgoing, relayed), "section", shards)
        return ((incoming, arriving, records), None)

    start = (blank_block, blank_block, jnp.zeros((MICRO * BLOCK, quarter), jnp.bfloat16))
    carry, _ = lax.scan(advance, start, jnp.arange(MICRO + cycle_size - 1, dtype=jnp.int32))
    kept = carry[2]
    for level in range(segment_bits):
        bit = shard_bits + segment_bits - 1 - level
        upper = index >> bit & 1
        halves = kept.reshape(kept.shape[0], 2, kept.shape[1] // 2)
        keep = jnp.where(upper == 1, halves[:, 1], halves[:, 0])
        send = jnp.where(upper == 1, halves[:, 0], halves[:, 1])
        received = partner(send, "section", bit)
        kept = (keep.astype(jnp.float32) + received.astype(jnp.float32)).astype(jnp.bfloat16)
    return kept


def solution(mesh):
    return jax.shard_map(
        body,
        mesh=mesh,
        in_specs=(
            P("section", "blk", None),
            P("blk"),
            P("blk"),
            P("section", "blk", None, None),
            P("section", None),
            P("section", None, None),
            P("section", None, None),
        ),
        out_specs=P("blk", "section"),
        check_vma=False,
    )
```

profile of v0, /device:TPU:0, one launch (start us, length us, event | category | flops | bytes accessed | tf_op | source)
XLA Modules:
  0.0 422.3 jit_solution(11661736484920512998)
XLA Ops:
  3.3 369.8 %while.17 = (s32[]{:T(128)}, bf16[64,4096]{1,0:T(8,128)(2,1)S(1)}, bf16[64,4096]{1,0:T(8,128)(2,1)S(1)}, bf16[512,4096]{1,0:T(8,128)(2,1)}, s32[9]{0:T(128)S(1)}...) while((s32[]{:T(128)}, bf16[64,4096]{1,0:T(8,128)(2,1)S(1)}, ...), condition=%wide.region_11.12_spmd.clone, body=%wide.region_0.11_spmd.clone.sunk | while | flops 1214793728 | bytes 34297604 | solution.py:164
  9.8 6.2 %conditional.9 = (f32[32]{0:T(128)S(1)}, f32[32]{0:T(128)S(1)}, f32[32,1280]{1,0:T(8,128)S(1)}, f32[32,1280]{1,0:T(8,128)S(1)}) conditional(s32[]{:T(128)} %convert_element_type.122, () %tuple.95, (bf16[64,4096]{1,0:T(8,128)(2,1)S(1)}, f32[4096]{0:T(1024)S(1)}, bf16[4096,1280]{1,0:T(8,128)(2,1)}) %tuple.96), branch_computations={%region_2.2_spmd, %region_3.4_spmd} | conditional | flops 672661440 | bytes 12534560 | solution.py:83
  10.1 5.9 %fusion.4 = f32[64,1280]{1,0:T(8,128)S(1)} fusion(bf16[4096,1280]{1,0:T(8,128)(2,1)} %get-tuple-element.392, bf16[64,4096]{1,0:T(8,128)(2,1)S(1)} %get-tuple-element.390, f32[4096]{0:T(1024)S(1)} %get-tuple-element.391), kind=kOutput, calls=%fused_computation.5 | convolution fusion | flops 671875072 | bytes 11354112 | tf_op jit(solution)/shard_map/while/body/eval_jaxpr/cond/branch_1_fun/dot_general | solution.py:73
  38.8 10.1 %collective-permute-done.3 = bf16[64,4096]{1,0:T(8,128)(2,1)S(1)} collective-permute-done((bf16[64,4096]{1,0:T(8,128)(2,1)S(1)}, bf16[64,4096]{1,0:T(8,128)(2,1)S(1)}, u32[]{:S(2)}, u32[]{:S(2)}) %collective-permute-start.3) | collective-permute-done | bytes 524320 | tf_op jit(solution)/shard_map/while/body/eval_jaxpr/ppermute | solution.py:23
  55.4 6.2 %conditional.9 = (f32[32]{0:T(128)S(1)}, f32[32]{0:T(128)S(1)}, f32[32,1280]{1,0:T(8,128)S(1)}, f32[32,1280]{1,0:T(8,128)S(1)}) conditional(s32[]{:T(128)} %convert_element_type.122, () %tuple.95, (bf16[64,4096]{1,0:T(8,128)(2,1)S(1)}, f32[4096]{0:T(1024)S(1)}, bf16[4096,1280]{1,0:T(8,128)(2,1)}) %tuple.96), branch_computations={%region_2.2_spmd, %region_3.4_spmd} | conditional | flops 672661440 | bytes 12534560 | solution.py:83
  55.6 5.9 %fusion.4 = f32[64,1280]{1,0:T(8,128)S(1)} fusion(bf16[4096,1280]{1,0:T(8,128)(2,1)} %get-tuple-element.392, bf16[64,4096]{1,0:T(8,128)(2,1)S(1)} %get-tuple-element.390, f32[4096]{0:T(1024)S(1)} %get-tuple-element.391), kind=kOutput, calls=%fused_computation.5 | convolution fusion | flops 671875072 | bytes 11354112 | tf_op jit(solution)/shard_map/while/body/eval_jaxpr/cond/branch_1_fun/dot_general | solution.py:73
  82.7 7.0 %collective-permute-done.3 = bf16[64,4096]{1,0:T(8,128)(2,1)S(1)} collective-permute-done((bf16[64,4096]{1,0:T(8,128)(2,1)S(1)}, bf16[64,4096]{1,0:T(8,128)(2,1)S(1)}, u32[]{:S(2)}, u32[]{:S(2)}) %collective-permute-start.3) | collective-permute-done | bytes 524320 | tf_op jit(solution)/shard_map/while/body/eval_jaxpr/ppermute | solution.py:23
  96.2 6.2 %conditional.9 = (f32[32]{0:T(128)S(1)}, f32[32]{0:T(128)S(1)}, f32[32,1280]{1,0:T(8,128)S(1)}, f32[32,1280]{1,0:T(8,128)S(1)}) conditional(s32[]{:T(128)} %convert_element_type.122, () %tuple.95, (bf16[64,4096]{1,0:T(8,128)(2,1)S(1)}, f32[4096]{0:T(1024)S(1)}, bf16[4096,1280]{1,0:T(8,128)(2,1)}) %tuple.96), branch_computations={%region_2.2_spmd, %region_3.4_spmd} | conditional | flops 672661440 | bytes 12534560 | solution.py:83
  96.4 5.9 %fusion.4 = f32[64,1280]{1,0:T(8,128)S(1)} fusion(bf16[4096,1280]{1,0:T(8,128)(2,1)} %get-tuple-element.392, bf16[64,4096]{1,0:T(8,128)(2,1)S(1)} %get-tuple-element.390, f32[4096]{0:T(1024)S(1)} %get-tuple-element.391), kind=kOutput, calls=%fused_computation.5 | convolution fusion | flops 671875072 | bytes 11354112 | tf_op jit(solution)/shard_map/while/body/eval_jaxpr/cond/branch_1_fun/dot_general | solution.py:73
  123.8 6.6 %collective-permute-done.3 = bf16[64,4096]{1,0:T(8,128)(2,1)S(1)} collective-permute-done((bf16[64,4096]{1,0:T(8,128)(2,1)S(1)}, bf16[64,4096]{1,0:T(8,128)(2,1)S(1)}, u32[]{:S(2)}, u32[]{:S(2)}) %collective-permute-start.3) | collective-permute-done | bytes 524320 | tf_op jit(solution)/shard_map/while/body/eval_jaxpr/ppermute | solution.py:23
  136.9 6.2 %conditional.9 = (f32[32]{0:T(128)S(1)}, f32[32]{0:T(128)S(1)}, f32[32,1280]{1,0:T(8,128)S(1)}, f32[32,1280]{1,0:T(8,128)S(1)}) conditional(s32[]{:T(128)} %convert_element_type.122, () %tuple.95, (bf16[64,4096]{1,0:T(8,128)(2,1)S(1)}, f32[4096]{0:T(1024)S(1)}, bf16[4096,1280]{1,0:T(8,128)(2,1)}) %tuple.96), branch_computations={%region_2.2_spmd, %region_3.4_spmd} | conditional | flops 672661440 | bytes 12534560 | solution.py:83
  137.1 5.9 %fusion.4 = f32[64,1280]{1,0:T(8,128)S(1)} fusion(bf16[4096,1280]{1,0:T(8,128)(2,1)} %get-tuple-element.392, bf16[64,4096]{1,0:T(8,128)(2,1)S(1)} %get-tuple-element.390, f32[4096]{0:T(1024)S(1)} %get-tuple-element.391), kind=kOutput, calls=%fused_computation.5 | convolution fusion | flops 671875072 | bytes 11354112 | tf_op jit(solution)/shard_map/while/body/eval_jaxpr/cond/branch_1_fun/dot_general | solution.py:73
  156.9 5.0 %conditional.11 = (bf16[64,4096]{1,0:T(8,128)(2,1)S(1)}) conditional(s32[]{:T(128)} %convert_element_type.122, bf16[64,4096]{1,0:T(8,128)(2,1)S(1)} %get-tuple-element.655, (pred[64]{0:T(512)(128)(4,1)S(1)}, bf16[64,4096]{1,0:T(8,128)(2,1)S(1)}, pred[]{:T(512)}, bf16[64,1024]{1,0:T(8,128)(2,1)S(1)}, bf16[64,1024]{1,0:T(8,128)(2,1)S(1)}, ...), branch_computations={%region_9.9_spmd, %region_10.10_spmd} | conditional | flops 537985024 | bytes 9699401 | solution.py:153
  164.5 6.6 %collective-permute-done.3 = bf16[64,4096]{1,0:T(8,128)(2,1)S(1)} collective-permute-done((bf16[64,4096]{1,0:T(8,128)(2,1)S(1)}, bf16[64,4096]{1,0:T(8,128)(2,1)S(1)}, u32[]{:S(2)}, u32[]{:S(2)}) %collective-permute-start.3) | collective-permute-done | bytes 524320 | tf_op jit(solution)/shard_map/while/body/eval_jaxpr/ppermute | solution.py:23
  177.7 6.2 %conditional.9 = (f32[32]{0:T(128)S(1)}, f32[32]{0:T(128)S(1)}, f32[32,1280]{1,0:T(8,128)S(1)}, f32[32,1280]{1,0:T(8,128)S(1)}) conditional(s32[]{:T(128)} %convert_element_type.122, () %tuple.95, (bf16[64,4096]{1,0:T(8,128)(2,1)S(1)}, f32[4096]{0:T(1024)S(1)}, bf16[4096,1280]{1,0:T(8,128)(2,1)}) %tuple.96), branch_computations={%region_2.2_spmd, %region_3.4_spmd} | conditional | flops 672661440 | bytes 12534560 | solution.py:83
  177.9 5.9 %fusion.4 = f32[64,1280]{1,0:T(8,128)S(1)} fusion(bf16[4096,1280]{1,0:T(8,128)(2,1)} %get-tuple-element.392, bf16[64,4096]{1,0:T(8,128)(2,1)S(1)} %get-tuple-element.390, f32[4096]{0:T(1024)S(1)} %get-tuple-element.391), kind=kOutput, calls=%fused_computation.5 | convolution fusion | flops 671875072 | bytes 11354112 | tf_op jit(solution)/shard_map/while/body/eval_jaxpr/cond/branch_1_fun/dot_general | solution.py:73
  197.6 5.0 %conditional.11 = (bf16[64,4096]{1,0:T(8,128)(2,1)S(1)}) conditional(s32[]{:T(128)} %convert_element_type.122, bf16[64,4096]{1,0:T(8,128)(2,1)S(1)} %get-tuple-element.655, (pred[64]{0:T(512)(128)(4,1)S(1)}, bf16[64,4096]{1,0:T(8,128)(2,1)S(1)}, pred[]{:T(512)}, bf16[64,1024]{1,0:T(8,128)(2,1)S(1)}, bf16[64,1024]{1,0:T(8,128)(2,1)S(1)}, ...), branch_computations={%region_9.9_spmd, %region_10.10_spmd} | conditional | flops 537985024 | bytes 9699401 | solution.py:153
  205.2 6.6 %collective-permute-done.3 = bf16[64,4096]{1,0:T(8,128)(2,1)S(1)} collective-permute-done((bf16[64,4096]{1,0:T(8,128)(2,1)S(1)}, bf16[64,4096]{1,0:T(8,128)(2,1)S(1)}, u32[]{:S(2)}, u32[]{:S(2)}) %collective-permute-start.3) | collective-permute-done | bytes 524320 | tf_op jit(solution)/shard_map/while/body/eval_jaxpr/ppermute | solution.py:23
  218.4 6.2 %conditional.9 = (f32[32]{0:T(128)S(1)}, f32[32]{0:T(128)S(1)}, f32[32,1280]{1,0:T(8,128)S(1)}, f32[32,1280]{1,0:T(8,128)S(1)}) conditional(s32[]{:T(128)} %convert_element_type.122, () %tuple.95, (bf16[64,4096]{1,0:T(8,128)(2,1)S(1)}, f32[4096]{0:T(1024)S(1)}, bf16[4096,1280]{1,0:T(8,128)(2,1)}) %tuple.96), branch_computations={%region_2.2_spmd, %region_3.4_spmd} | conditional | flops 672661440 | bytes 12534560 | solution.py:83
  218.6 5.9 %fusion.4 = f32[64,1280]{1,0:T(8,128)S(1)} fusion(bf16[4096,1280]{1,0:T(8,128)(2,1)} %get-tuple-element.392, bf16[64,4096]{1,0:T(8,128)(2,1)S(1)} %get-tuple-element.390, f32[4096]{0:T(1024)S(1)} %get-tuple-element.391), kind=kOutput, calls=%fused_computation.5 | convolution fusion | flops 671875072 | bytes 11354112 | tf_op jit(solution)/shard_map/while/body/eval_jaxpr/cond/branch_1_fun/dot_general | solution.py:73
  245.9 6.6 %collective-permute-done.3 = bf16[64,4096]{1,0:T(8,128)(2,1)S(1)} collective-permute-done((bf16[64,4096]{1,0:T(8,128)(2,1)S(1)}, bf16[64,4096]{1,0:T(8,128)(2,1)S(1)}, u32[]{:S(2)}, u32[]{:S(2)}) %collective-permute-start.3) | collective-permute-done | bytes 524320 | tf_op jit(solution)/shard_map/while/body/eval_jaxpr/ppermute | solution.py:23
  259.1 6.2 %conditional.9 = (f32[32]{0:T(128)S(1)}, f32[32]{0:T(128)S(1)}, f32[32,1280]{1,0:T(8,128)S(1)}, f32[32,1280]{1,0:T(8,128)S(1)}) conditional(s32[]{:T(128)} %convert_element_type.122, () %tuple.95, (bf16[64,4096]{1,0:T(8,128)(2,1)S(1)}, f32[4096]{0:T(1024)S(1)}, bf16[4096,1280]{1,0:T(8,128)(2,1)}) %tuple.96), branch_computations={%region_2.2_spmd, %region_3.4_spmd} | conditional | flops 672661440 | bytes 12534560 | solution.py:83
  259.3 5.9 %fusion.4 = f32[64,1280]{1,0:T(8,128)S(1)} fusion(bf16[4096,1280]{1,0:T(8,128)(2,1)} %get-tuple-element.392, bf16[64,4096]{1,0:T(8,128)(2,1)S(1)} %get-tuple-element.390, f32[4096]{0:T(1024)S(1)} %get-tuple-element.391), kind=kOutput, calls=%fused_computation.5 | convolution fusion | flops 671875072 | bytes 11354112 | tf_op jit(solution)/shard_map/while/body/eval_jaxpr/cond/branch_1_fun/dot_general | solution.py:73
  286.6 6.6 %collective-permute-done.3 = bf16[64,4096]{1,0:T(8,128)(2,1)S(1)} collective-permute-done((bf16[64,4096]{1,0:T(8,128)(2,1)S(1)}, bf16[64,4096]{1,0:T(8,128)(2,1)S(1)}, u32[]{:S(2)}, u32[]{:S(2)}) %collective-permute-start.3) | collective-permute-done | bytes 524320 | tf_op jit(solution)/shard_map/while/body/eval_jaxpr/ppermute | solution.py:23
  299.8 6.2 %conditional.9 = (f32[32]{0:T(128)S(1)}, f32[32]{0:T(128)S(1)}, f32[32,1280]{1,0:T(8,128)S(1)}, f32[32,1280]{1,0:T(8,128)S(1)}) conditional(s32[]{:T(128)} %convert_element_type.122, () %tuple.95, (bf16[64,4096]{1,0:T(8,128)(2,1)S(1)}, f32[4096]{0:T(1024)S(1)}, bf16[4096,1280]{1,0:T(8,128)(2,1)}) %tuple.96), branch_computations={%region_2.2_spmd, %region_3.4_spmd} | conditional | flops 672661440 | bytes 12534560 | solution.py:83
  300.0 5.9 %fusion.4 = f32[64,1280]{1,0:T(8,128)S(1)} fusion(bf16[4096,1280]{1,0:T(8,128)(2,1)} %get-tuple-element.392, bf16[64,4096]{1,0:T(8,128)(2,1)S(1)} %get-tuple-element.390, f32[4096]{0:T(1024)S(1)} %get-tuple-element.391), kind=kOutput, calls=%fused_computation.5 | convolution fusion | flops 671875072 | bytes 11354112 | tf_op jit(solution)/shard_map/while/body/eval_jaxpr/cond/branch_1_fun/dot_general | solution.py:73
  327.3 6.7 %collective-permute-done.3 = bf16[64,4096]{1,0:T(8,128)(2,1)S(1)} collective-permute-done((bf16[64,4096]{1,0:T(8,128)(2,1)S(1)}, bf16[64,4096]{1,0:T(8,128)(2,1)S(1)}, u32[]{:S(2)}, u32[]{:S(2)}) %collective-permute-start.3) | collective-permute-done | bytes 524320 | tf_op jit(solution)/shard_map/while/body/eval_jaxpr/ppermute | solution.py:23
  342.7 6.6 %collective-permute-start.4 = (bf16[64,4096]{1,0:T(8,128)(2,1)S(1)}, bf16[64,4096]{1,0:T(8,128)(2,1)S(1)}, u32[]{:S(2)}, u32[]{:S(2)}) collective-permute-start(bf16[64,4096]{1,0:T(8,128)(2,1)S(1)} %get-tuple-element.663), channel_id=1, source_target_pairs={{0,2},{1,3},{2,0},{3,1},{4,6},{5,7},{6,4},{7,5},{8,10},{9,11},{10,... | collective-permute-start | bytes 1572872 | tf_op jit(solution)/shard_map/while/body/eval_jaxpr/ppermute | solution.py:23
  353.8 12.2 %collective-permute-start.3 = (bf16[64,4096]{1,0:T(8,128)(2,1)S(1)}, bf16[64,4096]{1,0:T(8,128)(2,1)S(1)}, u32[]{:S(2)}, u32[]{:S(2)}) collective-permute-start(bf16[64,4096]{1,0:T(8,128)(2,1)S(1)} %get-tuple-element.757), channel_id=1, source_target_pairs={{0,2},{1,3},{2,0},{3,1},{4,6},{5,7},{6,4},{7,5},{8,10},{9,11},{10,... | collective-permute-start | bytes 1572872 | tf_op jit(solution)/shard_map/while/body/eval_jaxpr/ppermute | solution.py:23
  368.0 5.1 %collective-permute-done.3 = bf16[64,4096]{1,0:T(8,128)(2,1)S(1)} collective-permute-done((bf16[64,4096]{1,0:T(8,128)(2,1)S(1)}, bf16[64,4096]{1,0:T(8,128)(2,1)S(1)}, u32[]{:S(2)}, u32[]{:S(2)}) %collective-permute-start.3) | collective-permute-done | bytes 524320 | tf_op jit(solution)/shard_map/while/body/eval_jaxpr/ppermute | solution.py:23
  373.2 6.5 %copy.8 = bf16[512,4096]{0,1:T(8,128)(2,1)} copy(bf16[512,4096]{1,0:T(8,128)(2,1)} %get-tuple-element.438) | data formatting | bytes 8388608 | tf_op jit(solution)/shard_map/while | solution.py:164
  384.3 34.6 %collective-permute-done.5 = bf16[512,2048]{0,1:T(8,128)(2,1)S(1)} collective-permute-done((bf16[512,2048]{0,1:T(8,128)(2,1)S(1)}, bf16[512,2048]{0,1:T(8,128)(2,1)S(1)}, u32[]{:S(2)}, u32[]{:S(2)}) %collective-permute-start.5) | collective-permute-done | bytes 2097184 | tf_op jit(solution)/shard_map/ppermute | solution.py:17
  (357 shorter events, 277.3 us)
Async XLA Ops:
  16.1 7.3 %collective-permute-start = (f32[32,1280]{1,0:T(8,128)S(1)}, f32[32,1280]{1,0:T(8,128)S(1)}, u32[]{:S(2)}, u32[]{:S(2)}) collective-permute-start(f32[32,1280]{1,0:T(8,128)S(1)} %broadcast_select_fusion.7), channel_id=1, source_target_pairs={{0,1},{1,0},{2,3},{3,2},{4,5},{5,4},{6,7},{7,6},{8,9},{9,8},{10,11... | collective-permute-start | bytes 491528 | tf_op jit(solution)/shard_map/while/body/eval_jaxpr/ppermute | solution.py:17
  19.2 19.5 %collective-permute-start.4 = (bf16[64,4096]{1,0:T(8,128)(2,1)S(1)}, bf16[64,4096]{1,0:T(8,128)(2,1)S(1)}, u32[]{:S(2)}, u32[]{:S(2)}) collective-permute-start(bf16[64,4096]{1,0:T(8,128)(2,1)S(1)} %get-tuple-element.663), channel_id=1, source_target_pairs={{0,2},{1,3},{2,0},{3,1},{4,6},{5,7},{6,4},{7,5},{8,10},{9,11},{10,... | collective-permute-start | bytes 1572872 | tf_op jit(solution)/shard_map/while/body/eval_jaxpr/ppermute | solution.py:23
  27.3 4.3 %collective-permute-start.2 = (bf16[32,1024]{1,0:T(8,128)(2,1)S(1)}, bf16[32,1024]{1,0:T(8,128)(2,1)S(1)}, u32[]{:S(2)}, u32[]{:S(2)}) collective-permute-start(bf16[32,1024]{1,0:T(8,128)(2,1)S(1)} %get-tuple-element.756), channel_id=1, source_target_pairs={{0,1},{1,0},{2,3},{3,2},{4,5},{5,4},{6,7},{7,6},{8,9},{9,8},{10,11... | collective-permute-start | bytes 196616 | tf_op jit(solution)/shard_map/while/body/eval_jaxpr/ppermute | solution.py:17
  36.6 12.2 %collective-permute-start.3 = (bf16[64,4096]{1,0:T(8,128)(2,1)S(1)}, bf16[64,4096]{1,0:T(8,128)(2,1)S(1)}, u32[]{:S(2)}, u32[]{:S(2)}) collective-permute-start(bf16[64,4096]{1,0:T(8,128)(2,1)S(1)} %get-tuple-element.757), channel_id=1, source_target_pairs={{0,2},{1,3},{2,0},{3,1},{4,6},{5,7},{6,4},{7,5},{8,10},{9,11},{10,... | collective-permute-start | bytes 1572872 | tf_op jit(solution)/shard_map/while/body/eval_jaxpr/ppermute | solution.py:23
  61.6 5.5 %collective-permute-start = (f32[32,1280]{1,0:T(8,128)S(1)}, f32[32,1280]{1,0:T(8,128)S(1)}, u32[]{:S(2)}, u32[]{:S(2)}) collective-permute-start(f32[32,1280]{1,0:T(8,128)S(1)} %broadcast_select_fusion.7), channel_id=1, source_target_pairs={{0,1},{1,0},{2,3},{3,2},{4,5},{5,4},{6,7},{7,6},{8,9},{9,8},{10,11... | collective-permute-start | bytes 491528 | tf_op jit(solution)/shard_map/while/body/eval_jaxpr/ppermute | solution.py:17
  63.7 19.0 %collective-permute-start.4 = (bf16[64,4096]{1,0:T(8,128)(2,1)S(1)}, bf16[64,4096]{1,0:T(8,128)(2,1)S(1)}, u32[]{:S(2)}, u32[]{:S(2)}) collective-permute-start(bf16[64,4096]{1,0:T(8,128)(2,1)S(1)} %get-tuple-element.663), channel_id=1, source_target_pairs={{0,2},{1,3},{2,0},{3,1},{4,6},{5,7},{6,4},{7,5},{8,10},{9,11},{10,... | collective-permute-start | bytes 1572872 | tf_op jit(solution)/shard_map/while/body/eval_jaxpr/ppermute | solution.py:23
  70.9 4.3 %collective-permute-start.2 = (bf16[32,1024]{1,0:T(8,128)(2,1)S(1)}, bf16[32,1024]{1,0:T(8,128)(2,1)S(1)}, u32[]{:S(2)}, u32[]{:S(2)}) collective-permute-start(bf16[32,1024]{1,0:T(8,128)(2,1)S(1)} %get-tuple-element.756), channel_id=1, source_target_pairs={{0,1},{1,0},{2,3},{3,2},{4,5},{5,4},{6,7},{7,6},{8,9},{9,8},{10,11... | collective-permute-start | bytes 196616 | tf_op jit(solution)/shard_map/while/body/eval_jaxpr/ppermute | solution.py:17
  80.3 9.4 %collective-permute-start.3 = (bf16[64,4096]{1,0:T(8,128)(2,1)S(1)}, bf16[64,4096]{1,0:T(8,128)(2,1)S(1)}, u32[]{:S(2)}, u32[]{:S(2)}) collective-permute-start(bf16[64,4096]{1,0:T(8,128)(2,1)S(1)} %get-tuple-element.757), channel_id=1, source_target_pairs={{0,2},{1,3},{2,0},{3,1},{4,6},{5,7},{6,4},{7,5},{8,10},{9,11},{10,... | collective-permute-start | bytes 1572872 | tf_op jit(solution)/shard_map/while/body/eval_jaxpr/ppermute | solution.py:23
  102.5 5.5 %collective-permute-start = (f32[32,1280]{1,0:T(8,128)S(1)}, f32[32,1280]{1,0:T(8,128)S(1)}, u32[]{:S(2)}, u32[]{:S(2)}) collective-permute-start(f32[32,1280]{1,0:T(8,128)S(1)} %broadcast_select_fusion.7), channel_id=1, source_target_pairs={{0,1},{1,0},{2,3},{3,2},{4,5},{5,4},{6,7},{7,6},{8,9},{9,8},{10,11... | collective-permute-start | bytes 491528 | tf_op jit(solution)/shard_map/while/body/eval_jaxpr/ppermute | solution.py:17
  104.5 19.3 %collective-permute-start.4 = (bf16[64,4096]{1,0:T(8,128)(2,1)S(1)}, bf16[64,4096]{1,0:T(8,128)(2,1)S(1)}, u32[]{:S(2)}, u32[]{:S(2)}) collective-permute-start(bf16[64,4096]{1,0:T(8,128)(2,1)S(1)} %get-tuple-element.663), channel_id=1, source_target_pairs={{0,2},{1,3},{2,0},{3,1},{4,6},{5,7},{6,4},{7,5},{8,10},{9,11},{10,... | collective-permute-start | bytes 1572872 | tf_op jit(solution)/shard_map/while/body/eval_jaxpr/ppermute | solution.py:23
  111.7 4.3 %collective-permute-start.2 = (bf16[32,1024]{1,0:T(8,128)(2,1)S(1)}, bf16[32,1024]{1,0:T(8,128)(2,1)S(1)}, u32[]{:S(2)}, u32[]{:S(2)}) collective-permute-start(bf16[32,1024]{1,0:T(8,128)(2,1)S(1)} %get-tuple-element.756), channel_id=1, source_target_pairs={{0,1},{1,0},{2,3},{3,2},{4,5},{5,4},{6,7},{7,6},{8,9},{9,8},{10,11... | collective-permute-start | bytes 196616 | tf_op jit(solution)/shard_map/while/body/eval_jaxpr/ppermute | solution.py:17
  121.1 9.2 %collective-permute-start.3 = (bf16[64,4096]{1,0:T(8,128)(2,1)S(1)}, bf16[64,4096]{1,0:T(8,128)(2,1)S(1)}, u32[]{:S(2)}, u32[]{:S(2)}) collective-permute-start(bf16[64,4096]{1,0:T(8,128)(2,1)S(1)} %get-tuple-element.757), channel_id=1, source_target_pairs={{0,2},{1,3},{2,0},{3,1},{4,6},{5,7},{6,4},{7,5},{8,10},{9,11},{10,... | collective-permute-start | bytes 1572872 | tf_op jit(solution)/shard_map/while/body/eval_jaxpr/ppermute | solution.py:23
  143.2 5.6 %collective-permute-start = (f32[32,1280]{1,0:T(8,128)S(1)}, f32[32,1280]{1,0:T(8,128)S(1)}, u32[]{:S(2)}, u32[]{:S(2)}) collective-permute-start(f32[32,1280]{1,0:T(8,128)S(1)} %broadcast_select_fusion.7), channel_id=1, source_target_pairs={{0,1},{1,0},{2,3},{3,2},{4,5},{5,4},{6,7},{7,6},{8,9},{9,8},{10,11... | collective-permute-start | bytes 491528 | tf_op jit(solution)/shard_map/while/body/eval_jaxpr/ppermute | solution.py:17
  145.3 19.3 %collective-permute-start.4 = (bf16[64,4096]{1,0:T(8,128)(2,1)S(1)}, bf16[64,4096]{1,0:T(8,128)(2,1)S(1)}, u32[]{:S(2)}, u32[]{:S(2)}) collective-permute-start(bf16[64,4096]{1,0:T(8,128)(2,1)S(1)} %get-tuple-element.663), channel_id=1, source_target_pairs={{0,2},{1,3},{2,0},{3,1},{4,6},{5,7},{6,4},{7,5},{8,10},{9,11},{10,... | collective-permute-start | bytes 1572872 | tf_op jit(solution)/shard_map/while/body/eval_jaxpr/ppermute | solution.py:23
  161.9 9.2 %collective-permute-start.3 = (bf16[64,4096]{1,0:T(8,128)(2,1)S(1)}, bf16[64,4096]{1,0:T(8,128)(2,1)S(1)}, u32[]{:S(2)}, u32[]{:S(2)}) collective-permute-start(bf16[64,4096]{1,0:T(8,128)(2,1)S(1)} %get-tuple-element.757), channel_id=1, source_target_pairs={{0,2},{1,3},{2,0},{3,1},{4,6},{5,7},{6,4},{7,5},{8,10},{9,11},{10,... | collective-permute-start | bytes 1572872 | tf_op jit(solution)/shard_map/while/body/eval_jaxpr/ppermute | solution.py:23
  183.9 5.5 %collective-permute-start = (f32[32,1280]{1,0:T(8,128)S(1)}, f32[32,1280]{1,0:T(8,128)S(1)}, u32[]{:S(2)}, u32[]{:S(2)}) collective-permute-start(f32[32,1280]{1,0:T(8,128)S(1)} %broadcast_select_fusion.7), channel_id=1, source_target_pairs={{0,1},{1,0},{2,3},{3,2},{4,5},{5,4},{6,7},{7,6},{8,9},{9,8},{10,11... | collective-permute-start | bytes 491528 | tf_op jit(solution)/shard_map/while/body/eval_jaxpr/ppermute | solution.py:17
  186.0 19.2 %collective-permute-start.4 = (bf16[64,4096]{1,0:T(8,128)(2,1)S(1)}, bf16[64,4096]{1,0:T(8,128)(2,1)S(1)}, u32[]{:S(2)}, u32[]{:S(2)}) collective-permute-start(bf16[64,4096]{1,0:T(8,128)(2,1)S(1)} %get-tuple-element.663), channel_id=1, source_target_pairs={{0,2},{1,3},{2,0},{3,1},{4,6},{5,7},{6,4},{7,5},{8,10},{9,11},{10,... | collective-permute-start | bytes 1572872 | tf_op jit(solution)/shard_map/while/body/eval_jaxpr/ppermute | solution.py:23
  202.6 9.2 %collective-permute-start.3 = (bf16[64,4096]{1,0:T(8,128)(2,1)S(1)}, bf16[64,4096]{1,0:T(8,128)(2,1)S(1)}, u32[]{:S(2)}, u32[]{:S(2)}) collective-permute-start(bf16[64,4096]{1,0:T(8,128)(2,1)S(1)} %get-tuple-element.757), channel_id=1, source_target_pairs={{0,2},{1,3},{2,0},{3,1},{4,6},{5,7},{6,4},{7,5},{8,10},{9,11},{10,... | collective-permute-start | bytes 1572872 | tf_op jit(solution)/shard_map/while/body/eval_jaxpr/ppermute | solution.py:23
  224.6 5.5 %collective-permute-start = (f32[32,1280]{1,0:T(8,128)S(1)}, f32[32,1280]{1,0:T(8,128)S(1)}, u32[]{:S(2)}, u32[]{:S(2)}) collective-permute-start(f32[32,1280]{1,0:T(8,128)S(1)} %broadcast_select_fusion.7), channel_id=1, source_target_pairs={{0,1},{1,0},{2,3},{3,2},{4,5},{5,4},{6,7},{7,6},{8,9},{9,8},{10,11... | collective-permute-start | bytes 491528 | tf_op jit(solution)/shard_map/while/body/eval_jaxpr/ppermute | solution.py:17
  226.7 19.2 %collective-permute-start.4 = (bf16[64,4096]{1,0:T(8,128)(2,1)S(1)}, bf16[64,4096]{1,0:T(8,128)(2,1)S(1)}, u32[]{:S(2)}, u32[]{:S(2)}) collective-permute-start(bf16[64,4096]{1,0:T(8,128)(2,1)S(1)} %get-tuple-element.663), channel_id=1, source_target_pairs={{0,2},{1,3},{2,0},{3,1},{4,6},{5,7},{6,4},{7,5},{8,10},{9,11},{10,... | collective-permute-start | bytes 1572872 | tf_op jit(solution)/shard_map/while/body/eval_jaxpr/ppermute | solution.py:23
  243.3 9.2 %collective-permute-start.3 = (bf16[64,4096]{1,0:T(8,128)(2,1)S(1)}, bf16[64,4096]{1,0:T(8,128)(2,1)S(1)}, u32[]{:S(2)}, u32[]{:S(2)}) collective-permute-start(bf16[64,4096]{1,0:T(8,128)(2,1)S(1)} %get-tuple-element.757), channel_id=1, source_target_pairs={{0,2},{1,3},{2,0},{3,1},{4,6},{5,7},{6,4},{7,5},{8,10},{9,11},{10,... | collective-permute-start | bytes 1572872 | tf_op jit(solution)/shard_map/while/body/eval_jaxpr/ppermute | solution.py:23
  265.4 5.5 %collective-permute-start = (f32[32,1280]{1,0:T(8,128)S(1)}, f32[32,1280]{1,0:T(8,128)S(1)}, u32[]{:S(2)}, u32[]{:S(2)}) collective-permute-start(f32[32,1280]{1,0:T(8,128)S(1)} %broadcast_select_fusion.7), channel_id=1, source_target_pairs={{0,1},{1,0},{2,3},{3,2},{4,5},{5,4},{6,7},{7,6},{8,9},{9,8},{10,11... | collective-permute-start | bytes 491528 | tf_op jit(solution)/shard_map/while/body/eval_jaxpr/ppermute | solution.py:17
  267.5 19.2 %collective-permute-start.4 = (bf16[64,4096]{1,0:T(8,128)(2,1)S(1)}, bf16[64,4096]{1,0:T(8,128)(2,1)S(1)}, u32[]{:S(2)}, u32[]{:S(2)}) collective-permute-start(bf16[64,4096]{1,0:T(8,128)(2,1)S(1)} %get-tuple-element.663), channel_id=1, source_target_pairs={{0,2},{1,3},{2,0},{3,1},{4,6},{5,7},{6,4},{7,5},{8,10},{9,11},{10,... | collective-permute-start | bytes 1572872 | tf_op jit(solution)/shard_map/while/body/eval_jaxpr/ppermute | solution.py:23
  284.0 9.2 %collective-permute-start.3 = (bf16[64,4096]{1,0:T(8,128)(2,1)S(1)}, bf16[64,4096]{1,0:T(8,128)(2,1)S(1)}, u32[]{:S(2)}, u32[]{:S(2)}) collective-permute-start(bf16[64,4096]{1,0:T(8,128)(2,1)S(1)} %get-tuple-element.757), channel_id=1, source_target_pairs={{0,2},{1,3},{2,0},{3,1},{4,6},{5,7},{6,4},{7,5},{8,10},{9,11},{10,... | collective-permute-start | bytes 1572872 | tf_op jit(solution)/shard_map/while/body/eval_jaxpr/ppermute | solution.py:23
  306.1 5.5 %collective-permute-start = (f32[32,1280]{1,0:T(8,128)S(1)}, f32[32,1280]{1,0:T(8,128)S(1)}, u32[]{:S(2)}, u32[]{:S(2)}) collective-permute-start(f32[32,1280]{1,0:T(8,128)S(1)} %broadcast_select_fusion.7), channel_id=1, source_target_pairs={{0,1},{1,0},{2,3},{3,2},{4,5},{5,4},{6,7},{7,6},{8,9},{9,8},{10,11... | collective-permute-start | bytes 491528 | tf_op jit(solution)/shard_map/while/body/eval_jaxpr/ppermute | solution.py:17
  308.2 19.2 %collective-permute-start.4 = (bf16[64,4096]{1,0:T(8,128)(2,1)S(1)}, bf16[64,4096]{1,0:T(8,128)(2,1)S(1)}, u32[]{:S(2)}, u32[]{:S(2)}) collective-permute-start(bf16[64,4096]{1,0:T(8,128)(2,1)S(1)} %get-tuple-element.663), channel_id=1, source_target_pairs={{0,2},{1,3},{2,0},{3,1},{4,6},{5,7},{6,4},{7,5},{8,10},{9,11},{10,... | collective-permute-start | bytes 1572872 | tf_op jit(solution)/shard_map/while/body/eval_jaxpr/ppermute | solution.py:23
  324.7 9.2 %collective-permute-start.3 = (bf16[64,4096]{1,0:T(8,128)(2,1)S(1)}, bf16[64,4096]{1,0:T(8,128)(2,1)S(1)}, u32[]{:S(2)}, u32[]{:S(2)}) collective-permute-start(bf16[64,4096]{1,0:T(8,128)(2,1)S(1)} %get-tuple-element.757), channel_id=1, source_target_pairs={{0,2},{1,3},{2,0},{3,1},{4,6},{5,7},{6,4},{7,5},{8,10},{9,11},{10,... | collective-permute-start | bytes 1572872 | tf_op jit(solution)/shard_map/while/body/eval_jaxpr/ppermute | solution.py:23
  340.6 8.7 %collective-permute-start = (f32[32,1280]{1,0:T(8,128)S(1)}, f32[32,1280]{1,0:T(8,128)S(1)}, u32[]{:S(2)}, u32[]{:S(2)}) collective-permute-start(f32[32,1280]{1,0:T(8,128)S(1)} %broadcast_select_fusion.7), channel_id=1, source_target_pairs={{0,1},{1,0},{2,3},{3,2},{4,5},{5,4},{6,7},{7,6},{8,9},{9,8},{10,11... | collective-permute-start | bytes 491528 | tf_op jit(solution)/shard_map/while/body/eval_jaxpr/ppermute | solution.py:17
  342.5 6.8 %collective-permute-start.1 = (f32[32]{0:T(128)S(1)}, f32[32]{0:T(128)S(1)}, u32[]{:S(2)}, u32[]{:S(2)}) collective-permute-start(f32[32]{0:T(128)S(1)} %broadcast_select_fusion.8), channel_id=1, source_target_pairs={{0,1},{1,0},{2,3},{3,2},{4,5},{5,4},{6,7},{7,6},{8,9},{9,8},{10,11... | collective-permute-start | bytes 392 | tf_op jit(solution)/shard_map/while/body/eval_jaxpr/ppermute | solution.py:17
  342.7 25.3 %collective-permute-start.4 = (bf16[64,4096]{1,0:T(8,128)(2,1)S(1)}, bf16[64,4096]{1,0:T(8,128)(2,1)S(1)}, u32[]{:S(2)}, u32[]{:S(2)}) collective-permute-start(bf16[64,4096]{1,0:T(8,128)(2,1)S(1)} %get-tuple-element.663), channel_id=1, source_target_pairs={{0,2},{1,3},{2,0},{3,1},{4,6},{5,7},{6,4},{7,5},{8,10},{9,11},{10,... | collective-permute-start | bytes 1572872 | tf_op jit(solution)/shard_map/while/body/eval_jaxpr/ppermute | solution.py:23
  353.8 19.4 %collective-permute-start.3 = (bf16[64,4096]{1,0:T(8,128)(2,1)S(1)}, bf16[64,4096]{1,0:T(8,128)(2,1)S(1)}, u32[]{:S(2)}, u32[]{:S(2)}) collective-permute-start(bf16[64,4096]{1,0:T(8,128)(2,1)S(1)} %get-tuple-element.757), channel_id=1, source_target_pairs={{0,2},{1,3},{2,0},{3,1},{4,6},{5,7},{6,4},{7,5},{8,10},{9,11},{10,... | collective-permute-start | bytes 1572872 | tf_op jit(solution)/shard_map/while/body/eval_jaxpr/ppermute | solution.py:23
  382.3 36.7 %collective-permute-start.5 = (bf16[512,2048]{0,1:T(8,128)(2,1)S(1)}, bf16[512,2048]{0,1:T(8,128)(2,1)S(1)}, u32[]{:S(2)}, u32[]{:S(2)}) collective-permute-start(bf16[512,2048]{0,1:T(8,128)(2,1)S(1)} %select_bitcast_fusion), channel_id=1, source_target_pairs={{0,2},{1,3},{2,0},{3,1},{4,6},{5,7},{6,4},{7,5},{8,10},{9,11},{10,... | collective-permute-start | bytes 6291464 | tf_op jit(solution)/shard_map/ppermute | solution.py:17
  (16 other events, 98.7 us)
where the time goes:
time: 425 us; the launch traced here: 422 us
  waiting for transfers between devices  143 us (34%)
  matrix products  107 us (25%)
  starting transfers between devices  64.2 us (15%)
  other arithmetic  47.3 us (11%)
  loops' own time  36.2 us (9%)
  local copies, waits for them, and re-layouts  24.1 us (6%)
    ppermute x28, waiting for transfers between devices, partner(): lax.ppermute(value, axis, [(i, i ^ 1 << distance) for i in range(lax.axis...  81.2 us
    ppermute x18, waiting for transfers between devices, shifted(): return lax.ppermute(value, axis, pairs)  62 us
    dot_general x8, matrix products, local_partials(): jnp.dot(scaled, proj_weight, preferred_element_type=jnp.float32)  47.2 us
    dot_general x8, matrix products, local_update(): jnp.dot(collected, out_weight, preferred_element_type=jnp.float32)  40.1 us
    ppermute x28, starting transfers between devices, partner(): lax.ppermute(value, axis, [(i, i ^ 1 << distance) for i in range(lax.axis...  38.2 us
    another operation x1, loops' own time, body(): lax.scan(advance, start, jnp.arange(MICRO + cycle_size - 1, dtype=jnp.int...  35 us
    ppermute x18, starting transfers between devices, shifted(): return lax.ppermute(value, axis, pairs)  26 us
    dynamic_update_slice x9, other arithmetic, advance(): lax.dynamic_update_slice_in_dim(records, jnp.where(leaving[:, None], outg...  18.3 us
  transfers between devices with their start and end apart: 46, of which 27 were waited for; matrix products, arithmetic and copies ran while one was open for 21% of the time, Pallas kernels for 0%

commit v1 on v0

--- a/solution.py
+++ b/solution.py
@@ -1,9 +1,13 @@
+import functools
 import math
 
 import jax
 import jax.numpy as jnp
 from jax import lax
+from jax.experimental import pallas as pl
+from jax.experimental.pallas import tpu as pltpu
 from jax.sharding import PartitionSpec as P
+
 
 BLOCK = 64
 MICRO = 8
@@ -174,9 +178,636 @@
     return kept
 
 
+CAPACITY = 40
+LIMIT = 10 * 1024 * 1024
+IN_VMEM = pl.BlockSpec(memory_space=pltpu.VMEM)
+IN_SMEM = pl.BlockSpec(memory_space=pltpu.SMEM)
+IN_HBM = pl.BlockSpec(memory_space=pltpu.HBM)
+
+
+def call(kernel, inputs, in_specs, outs, out_specs=None, scratch=(), flops=10**8, **more):
+    return pl.pallas_call(
+        kernel,
+        in_specs=in_specs,
+        out_specs=[IN_VMEM] * len(outs) if out_specs is None else out_specs,
+        out_shape=outs,
+        scratch_shapes=scratch,
+        compiler_params=pltpu.CompilerParams(vmem_limit_bytes=LIMIT),
+        cost_estimate=pl.CostEstimate(flops=flops, bytes_accessed=10**6, transcendentals=0),
+        **more,
+    )(*inputs)
+
+
+def seat():
+    index = lax.axis_index("section")
+    return index // 2, index % 2
+
+
+def chunk_blocks(chunk):
+    first = 4 * (chunk % 2) + chunk // 2
+    return first, first + 2
+
+
+def same_group(shape):
+    half = BLOCK // 2
+    first = lax.broadcasted_iota(jnp.int32, shape, 0)
+    second = lax.broadcasted_iota(jnp.int32, shape, 1)
+    return (first // half) % 2 == (second // half) % 2, first, second
+
+
+def chunk_rows(values):
+    lanes = lax.broadcasted_iota(jnp.int32, (1, 2 * BLOCK), 1)
+    rows = []
+    for chunk in range(4):
+        upper_row = values[2 * (chunk % 2) : 2 * (chunk % 2) + 1]
+        lower_row = values[2 * (chunk % 2) + 1 : 2 * (chunk % 2) + 2]
+        if chunk < 2:
+            rows.append(jnp.where(lanes < BLOCK, upper_row, pltpu.roll(lower_row, BLOCK, 1)))
+        else:
+            rows.append(jnp.where(lanes < BLOCK, pltpu.roll(upper_row, BLOCK, 1), lower_row))
+    return jnp.concatenate(rows + rows, axis=0)
+
+
+def exact_dot(a, b):
+    return jnp.dot(
+        a.astype(jnp.bfloat16), b.astype(jnp.bfloat16), preferred_element_type=jnp.float32
+    )
+
+
+def split_kernel(x_ref, *refs):
+    outs, sem = refs[:-1], refs[-1]
+    tall = outs[0].shape[0]
+    copies = [
+        pltpu.make_async_copy(x_ref.at[pl.ds(i * tall, tall)], out, sem.at[i])
+        for i, out in enumerate(outs)
+    ]
+    for copy in copies:
+        copy.start()
+    for copy in copies:
+        copy.wait()
+
+
+def prepare_kernel(exit_ref, length_ref, order_ref, active_ref, limit_ref, fit_ref):
+    upper, shard = seat()
+    tall = 2 * BLOCK
+    half = BLOCK // 2
+    values = chunk_rows(exit_ref[...].astype(jnp.float32))
+    deep = (values > 1).astype(jnp.float32)
+    same, first, second = same_group((tall, tall))
+    same = same.astype(jnp.float32)
+    ahead = jnp.where(first <= second, same, 0.0)
+    counts = exact_dot(deep, same)
+    fit_ref[0] = (jnp.max(counts) <= float(CAPACITY)).astype(jnp.int32)
+    rank = jnp.where(
+        deep > 0, exact_dot(deep, ahead) - 1, counts + exact_dot(1 - deep, ahead) - 1
+    )
+    lanes = lax.broadcasted_iota(jnp.int32, rank.shape, 1)
+    target = rank.astype(jnp.int32) + ((lanes // half) % 2) * BLOCK
+    for chunk in range(4):
+        order = first == target[chunk : chunk + 1]
+        order_ref[chunk] = order.astype(jnp.float32).astype(jnp.bfloat16)
+        natural = (first == second) & (values[chunk : chunk + 1] > 0)
+        ranked = order & (deep[chunk : chunk + 1] > 0)
+        chosen = jnp.where(
+            upper == 0, natural.astype(jnp.float32), ranked.astype(jnp.float32)
+        )
+        column = jnp.sum(chosen, axis=1, keepdims=True)
+        active_ref[chunk] = jnp.broadcast_to(column, (tall, 128))
+    context = limit_ref.shape[2] // half
+    lengths = length_ref[...].astype(jnp.float32)
+    lengths = jnp.concatenate([lengths, lengths], axis=0)
+    source = lax.broadcasted_iota(jnp.int32, (tall, limit_ref.shape[2]), 0)
+    column = lax.broadcasted_iota(jnp.int32, (tall, limit_ref.shape[2]), 1)
+    for parity in range(2):
+        spread = source == parity * BLOCK + shard * half + column // context
+        limit_ref[parity] = exact_dot(lengths, spread.astype(jnp.float32))
+
+
+def framed(pieces, height):
+    rows = []
+    for piece in pieces:
+        piece = piece.astype(jnp.float32)
+        rows.append(piece)
+        if piece.shape[0] < height:
+            rows.append(jnp.zeros((height - piece.shape[0], piece.shape[1]), jnp.float32))
+    return jnp.concatenate(rows, axis=0)
+
+
+def own_rows(upper, shard, piece, rows):
+    half = BLOCK // 2
+    base = jnp.where(upper == 0, piece * BLOCK + shard * half, shard * BLOCK + piece * half)
+    return pl.ds(pl.multiple_of(base, half), rows)
+
+
+def project_kernel(roles, load, *refs):
+    refs = list(refs)
+    x_ref = refs.pop(0) if roles != "upper" else None
+    a_ref = refs.pop(0) if roles != "lower" else None
+    gain_ref, w_ref = refs.pop(0), refs.pop(0)
+    if load == "second":
+        other_ref, cache_ref = refs.pop(0), refs.pop(0)
+    keep_ref, keep_sq_ref, send_ref = refs.pop(0), refs.pop(0), refs.pop(0)
+    if load:
+        held_ref, sem = refs.pop(0), refs.pop()
+    if load == "second":
+        held_cache_ref = refs.pop(0)
+    xs_ref, acc_ref, sq_ref = refs
+    upper, shard = seat()
+    features = w_ref.shape[0]
+    pieces = 4
+    depth = features // pieces
+    copies = []
+    if load == "first":
+        copies = [
+            pltpu.make_async_copy(
+                w_ref.at[pl.ds(i * depth, depth)], held_ref.at[pl.ds(i * depth, depth)], sem.at[i]
+            )
+            for i in range(pieces)
+        ]
+    elif load == "second":
+        copies = [
+            pltpu.make_async_copy(other_ref, held_ref, sem.at[0]),
+            pltpu.make_async_copy(cache_ref, held_cache_ref, sem.at[1]),
+        ]
+    for copy in copies:
+        copy.start()
+
+    def scale(read):
+        squares = None
+        for i in range(pieces):
+            columns = slice(i * depth, (i + 1) * depth)
+            x = read(columns)
+            for lane in range(0, depth, 128):
+                part = x[:, lane : lane + 128]
+                squares = part * part if squares is None else squares + part * part
+            xs_ref[:, columns] = (x * gain_ref[:, columns].astype(jnp.float32)).astype(jnp.bfloat16)
+        sq_ref[...] = squares
+
+    if roles != "upper":
+        @pl.when(upper == 0)
+        def _():
+            scale(lambda columns: x_ref[:, columns].astype(jnp.float32))
+
+    if roles != "lower":
+        @pl.when(upper != 0)
+        def _():
+            scale(lambda columns: framed([a_ref[g, :, columns] for g in range(2)], BLOCK))
+
+    def multiply():
+        if load == "first":
+            for i in range(pieces):
+                columns = slice(i * depth, (i + 1) * depth)
+                copies[i].wait()
+                product = jnp.dot(
+                    xs_ref[:, columns], held_ref[columns, :], preferred_element_type=jnp.float32
+                )
+                if i == 0:
+                    acc_ref[...] = product
+                else:
+                    acc_ref[...] += product
+        else:
+            acc_ref[...] = jnp.dot(xs_ref[...], w_ref[...], preferred_element_type=jnp.float32)
+        half = BLOCK // 2
+        width = keep_ref.shape[1]
+        for piece in range(2):
+            here = own_rows(upper, shard, piece, half)
+            there = own_rows(upper, 1 - shard, piece, half)
+            rows = pl.ds(piece * half, half)
+            keep_ref[rows, :] = acc_ref[here, :]
+            send_ref[rows, :width] = acc_ref[there, :].astype(jnp.bfloat16)
+            own = jnp.sum(sq_ref[here, :], axis=1, keepdims=True)
+            keep_sq_ref[rows, :] = jnp.broadcast_to(own, (half, 128))
+            other = jnp.broadcast_to(jnp.sum(sq_ref[there, :], axis=1, keepdims=True), (half, 128))
+            high = other.astype(jnp.bfloat16).astype(jnp.float32)
+            lanes = lax.broadcasted_iota(jnp.int32, (half, 128), 1)
+            send_ref[rows, width:] = jnp.where(lanes < 64, high, other - high).astype(jnp.bfloat16)
+
+    if load == "first":
+        multiply()
+    elif roles == "both":
+        multiply()
+    else:
+        pl.when((upper == 0) if roles == "lower" else (upper != 0))(multiply)
+    if load == "second":
+        for copy in copies:
+            copy.wait()
+
+
+def project(roles, x, a, gain, w, load=None, other=None, cache=None):
+    features, width = w.shape
+    tall = 2 * BLOCK
+    inputs = [x] * (roles != "upper") + [a] * (roles != "lower") + [gain, w]
+    specs = [IN_VMEM] * len(inputs)
+    outs = [
+        pltpu.VMEM((BLOCK, width), jnp.float32),
+        pltpu.VMEM((BLOCK, 128), jnp.float32),
+        pltpu.VMEM((BLOCK, width + 128), jnp.bfloat16),
+    ]
+    scratch = [
+        pltpu.VMEM((tall, features), jnp.bfloat16),
+        pltpu.VMEM((tall, width), jnp.float32),
+        pltpu.VMEM((tall, 128), jnp.float32),
+    ]
+    if load == "first":
+        specs[-1] = IN_HBM
+        outs.append(pltpu.VMEM(w.shape, w.dtype))
+        scratch.append(pltpu.SemaphoreType.DMA((4,)))
+    elif load == "second":
+        inputs += [other, cache]
+        specs += [IN_HBM, IN_HBM]
+        outs += [pltpu.VMEM(other.shape, other.dtype), pltpu.VMEM(cache.shape, cache.dtype)]
+        scratch.append(pltpu.SemaphoreType.DMA((2,)))
+    return call(
+        functools.partial(project_kernel, roles, load), inputs, specs, outs, scratch=scratch,
+        flops=2 * tall * features * width,
+    )
+
+
+def by_role(roles, upper, lower_part, upper_part):
+    if roles == "both":
+        pl.when(upper == 0)(lower_part)
+        pl.when(upper != 0)(upper_part)
+    elif roles == "lower":
+        lower_part()
+    else:
+        upper_part()
+
+
+def attend_kernel(roles, low, high, total_width, keep_ref, keep_sq_ref, recv_ref, kv_ref, limit_ref, order_ref, out_ref,
+                  fit_ref, wide_ref, att_ref, spread_ref):
+    upper, shard = seat()
+    if roles != "both":
+        pl.when((upper == 0) if roles == "lower" else (upper != 0))(
+            functools.partial(
+                attend_rows, roles, low if roles == "lower" else high, total_width, upper, shard, keep_ref, keep_sq_ref,
+                recv_ref, kv_ref, limit_ref, order_ref, out_ref, fit_ref, wide_ref, att_ref, spread_ref,
+            )
+        )
+    else:
+        attend_rows(
+            roles, jnp.where(upper == 0, low, high), total_width, upper, shard, keep_ref, keep_sq_ref,
+            recv_ref, kv_ref, limit_ref, order_ref, out_ref, fit_ref, wide_ref, att_ref, spread_ref,
+        )
+
+
+def attend_rows(roles, chunk, total_width, upper, shard, keep_ref, keep_sq_ref, recv_ref, kv_ref, limit_ref, order_ref,
+                out_ref, fit_ref, wide_ref, att_ref, spread_ref):
+    width = keep_ref.shape[1]
+    query_width = out_ref.shape[1]
+    context = kv_ref.shape[1]
+    head_size = kv_ref.shape[2] // 2
+    heads = query_width // head_size
+    half = BLOCK // 2
+    tokens = 16
+    columns = tokens * context
+    other = recv_ref[:, width:].astype(jnp.float32)
+    squares = keep_sq_ref[:, :1] + other[:, :1] + other[:, 64:65]
+    factor = lax.rsqrt(squares / total_width + EPSILON)
+    fitted = (keep_ref[...] + recv_ref[:, :width].astype(jnp.float32)) * factor
+    scale = 1.0 / math.sqrt(head_size)
+    rounded = jnp.concatenate(
+        [
+            (fitted[:, :query_width] * scale).astype(jnp.bfloat16),
+            fitted[:, query_width:].astype(jnp.bfloat16),
+        ],
+        axis=1,
+    )
+
+    def natural():
+        fit_ref[...] = rounded
+
+    def restored():
+        own_order = order_ref[chunk, pl.ds(pl.multiple_of(shard * BLOCK, BLOCK), BLOCK), :]
+        wide_ref[...] = lax.dot_general(
+            own_order, rounded, (((0,), (0,)), ((), ())), preferred_element_type=jnp.float32
+        )
+        for piece in range(2):
+            rows = pl.ds(pl.multiple_of(piece * BLOCK + shard * half, half), half)
+            fit_ref[piece * half : (piece + 1) * half, :] = wide_ref[rows, :].astype(jnp.bfloat16)
+
+    by_role(roles, upper, natural, restored)
+    row = lax.broadcasted_iota(jnp.int32, (heads * tokens, columns), 0)
+    column = lax.broadcasted_iota(jnp.int32, (heads * tokens, columns), 1)
+    same = (row % tokens) == (column // context)
+    position = (lax.broadcasted_iota(jnp.int32, (1, columns), 1) % context).astype(jnp.float32)
+    parity = chunk // 2
+    first_row = 2 * (chunk % 2)
+    pieces = [(block, part) for block in range(2) for part in range(half // tokens)]
+    queries, scores, owns, masks, tops, raws, raw_owns, totals = [], [], [], [], [], [], [], []
+
+    def cache_rows(block, part):
+        first = (2 * (first_row + block) + parity) * half + part * tokens
+        return pl.ds(pl.multiple_of(first, tokens), tokens)
+
+    for block, part in pieces:
+        base = block * half + part * tokens
+        rows = slice(base, base + tokens)
+        queries.append(
+            jnp.concatenate(
+                [fit_ref[rows, h * head_size : (h + 1) * head_size] for h in range(heads)], axis=0
+            )
+        )
+    for i, (block, part) in enumerate(pieces):
+        rows = slice(block * half + part * tokens, block * half + (part + 1) * tokens)
+        keys = kv_ref[cache_rows(block, part), :, :head_size].reshape(columns, head_size)
+        scores.append(
+            lax.dot_general(
+                queries[i], keys, (((1,), (1,)), ((), ())), preferred_element_type=jnp.float32
+            )
+        )
+        key_new = fit_ref[rows, query_width : query_width + head_size].astype(jnp.float32)
+        key_new = jnp.concatenate([key_new] * heads, axis=0)
+        owns.append(jnp.sum(queries[i].astype(jnp.float32) * key_new, axis=1, keepdims=True))
+    for i, (block, part) in enumerate(pieces):
+        limit = limit_ref[parity, pl.ds(first_row + block, 1), part * columns : (part + 1) * columns]
+        masks.append(same & (position < limit))
+        scores[i] = jnp.where(masks[i], scores[i], NEGATIVE)
+        tops.append(jnp.maximum(jnp.max(scores[i], axis=1, keepdims=True), owns[i]))
+    for i in range(len(pieces)):
+        raws.append(jnp.where(masks[i], jnp.exp(scores[i] - tops[i]), 0.0))
+        raw_owns.append(jnp.exp(owns[i] - tops[i]))
+        totals.append(jnp.sum(raws[i], axis=1, keepdims=True) + raw_owns[i])
+    for i, (block, part) in enumerate(pieces):
+        rows = slice(block * half + part * tokens, block * half + (part + 1) * tokens)
+        values = kv_ref[cache_rows(block, part), :, head_size:].reshape(columns, head_size)
+        weights = (raws[i] / totals[i]).astype(jnp.bfloat16)
+        own_weight = (raw_owns[i] / totals[i]).astype(jnp.bfloat16).astype(jnp.float32)
+        value_new = fit_ref[rows, query_width + head_size :].astype(jnp.float32)
+        value_new = jnp.concatenate([value_new] * heads, axis=0)
+        attended = jnp.dot(weights, values, preferred_element_type=jnp.float32)
+        attended = (attended + own_weight * value_new).astype(jnp.bfloat16)
+        for h in range(heads):
+            att_ref[rows, h * head_size : (h + 1) * head_size] = attended[
+                h * tokens : (h + 1) * tokens
+            ]
+
+    def kept():
+        out_ref[...] = att_ref[...]
+
+    def ranked():
+        spread_ref[...] = jnp.zeros_like(spread_ref)
+        for piece in range(2):
+            rows = pl.ds(pl.multiple_of(piece * BLOCK + shard * half, half), half)
+            spread_ref[rows, :] = att_ref[piece * half : (piece + 1) * half, :]
+        own_order = order_ref[chunk, pl.ds(pl.multiple_of(shard * BLOCK, BLOCK), BLOCK), :]
+        out_ref[...] = jnp.dot(
+            own_order, spread_ref[...], preferred_element_type=jnp.float32
+        ).astype(jnp.bfloat16)
+
+    by_role(roles, upper, kept, ranked)
+
+
+def attend(roles, low, high, total_width, keep, keep_sq, recv, kv, limits, order, query_width):
+    width = keep.shape[1]
+    tall = 2 * BLOCK
+    return call(
+        functools.partial(attend_kernel, roles, low, high, total_width),
+        [keep, keep_sq, recv, kv, limits, order], [IN_VMEM] * 6,
+        [pltpu.VMEM((BLOCK, query_width), jnp.bfloat16)],
+        scratch=[
+            pltpu.VMEM((BLOCK, width), jnp.bfloat16),
+            pltpu.VMEM((tall, width), jnp.float32),
+            pltpu.VMEM((BLOCK, query_width), jnp.bfloat16),
+            pltpu.VMEM((tall, query_width), jnp.bfloat16),
+        ],
+        flops=900_000_000,
+    )[0]
+
+
+def output_kernel(roles, low, high, *refs):
+    refs = list(refs)
+    own_ref, recv_ref, active_ref, order_ref = refs[:4]
+    refs = refs[4:]
+    x_ref = refs.pop(0) if roles != "upper" else None
+    a_ref = refs.pop(0) if roles != "lower" else None
+    w_ref = refs.pop(0)
+    if roles != "upper":
+        up_ref, high_rest_ref, low_rest_ref = refs[:3]
+        refs = refs[3:]
+    if roles != "lower":
+        low_ref, high_ref = refs[:2]
+        refs = refs[2:]
+    (att_ref,) = refs
+    upper, shard = seat()
+    chunk = jnp.where(upper == 0, low, high)
+    half = BLOCK // 2
+    tile = 512
+    features = w_ref.shape[1]
+    middle = features // 2
+
+    def gather():
+        for piece in range(2):
+            rows = pl.ds(piece * half, half)
+            att_ref[own_rows(upper, shard, piece, half), :] = own_ref[rows, :]
+            att_ref[own_rows(upper, 1 - shard, piece, half), :] = recv_ref[rows, :]
+
+    def updated(columns, state):
+        branch = jnp.dot(att_ref[...], w_ref[:, columns], preferred_element_type=jnp.float32)
+        active = active_ref[chunk][:, :1] > 0
+        return jnp.where(active, state + branch, state)
+
+    if roles != "upper":
+        @pl.when(upper == 0)
+        def _():
+            gather()
+            order = order_ref[low]
+
+            def each(i, carry):
+                inner = pl.ds(pl.multiple_of(i * tile, tile), tile)
+                for side, rest_ref in enumerate((low_rest_ref, high_rest_ref)):
+                    columns = pl.ds(pl.multiple_of(i * tile + side * middle, tile), tile)
+                    state = updated(columns, x_ref[:, columns].astype(jnp.float32))
+                    sorted_rows = jnp.dot(
+                        order, state.astype(jnp.bfloat16), preferred_element_type=jnp.float32
+                    )
+                    for g in range(2):
+                        top = g * BLOCK
+                        up_ref[g, :, columns] = sorted_rows[top : top + CAPACITY].astype(jnp.bfloat16)
+                        rest_ref[g, :, inner] = sorted_rows[top + CAPACITY : top + BLOCK].astype(jnp.bfloat16)
+                return carry
+
+            lax.fori_loop(0, middle // tile, each, 0)
+
+    if roles != "lower":
+        @pl.when(upper != 0)
+        def _():
+            gather()
+
+            def each(i, carry):
+                inner = pl.ds(pl.multiple_of(i * tile, tile), tile)
+                for side, half_ref in enumerate((low_ref, high_ref)):
+                    columns = pl.ds(pl.multiple_of(i * tile + side * middle, tile), tile)
+                    state = updated(columns, framed([a_ref[g, :, columns] for g in range(2)], BLOCK))
+                    for g in range(2):
+                        top = g * BLOCK
+                        half_ref[g, :, inner] = state[top : top + CAPACITY].astype(jnp.bfloat16)
+                return carry
+
+            lax.fori_loop(0, middle // tile, each, 0)
+
+
+def output(roles, low, high, own, recv, active, order, x, a, w):
+    depth, features = w.shape
+    middle = features // 2
+    inputs = [own, recv, active, order] + [x] * (roles != "upper") + [a] * (roles != "lower") + [w]
+    rest = BLOCK - CAPACITY
+    outs = []
+    if roles != "upper":
+        outs += [
+            pltpu.VMEM((2, CAPACITY, features), jnp.bfloat16),
+            pltpu.VMEM((2, rest, middle), jnp.bfloat16),
+            pltpu.VMEM((2, rest, middle), jnp.bfloat16),
+        ]
+    if roles != "lower":
+        outs += [pltpu.VMEM((2, CAPACITY, middle), jnp.bfloat16)] * 2
+    return call(
+        functools.partial(output_kernel, roles, low, high), inputs, [IN_VMEM] * len(inputs), outs,
+        scratch=[pltpu.VMEM((2 * BLOCK, depth), jnp.bfloat16)],
+        flops=4 * BLOCK * features * depth,
+    )
+
+
+def settle_kernel(chunk, fresh, *refs):
+    order_ref, d_ref, own_rest_ref, own_high_ref, recv_rest_ref = refs[:5]
+    refs = refs[5:] if fresh else refs[6:]
+    out_ref, rows_ref, sem = refs
+    upper, _ = seat()
+    order = order_ref[chunk]
+    tile = 512
+
+    def place(first, rest):
+        for start in range(0, rows_ref.shape[1], tile):
+            columns = slice(start, start + tile)
+            pieces = []
+            for g in range(2):
+                pieces += [
+                    first[g, :, columns].astype(jnp.float32),
+                    rest[g, :, columns].astype(jnp.float32),
+                ]
+            frame = jnp.concatenate(pieces, axis=0).astype(jnp.bfloat16)
+            rows_ref[:, columns] = lax.dot_general(
+                order, frame, (((0,), (0,)), ((), ())), preferred_element_type=jnp.float32
+            ).astype(jnp.bfloat16)
+
+    @pl.when(upper == 0)
+    def _():
+        place(d_ref, own_rest_ref)
+
+    @pl.when(upper != 0)
+    def _():
+        place(own_high_ref, recv_rest_ref)
+
+    copies = [
+        pltpu.make_async_copy(
+            rows_ref.at[pl.ds(i * BLOCK, BLOCK)], out_ref.at[pl.ds(block * BLOCK, BLOCK)], sem.at[i]
+        )
+        for i, block in enumerate(chunk_blocks(chunk))
+    ]
+    for copy in copies:
+        copy.start()
+    for copy in copies:
+        copy.wait()
+
+
+def settle(chunk, order, d, own_rest, own_high, recv_rest, out):
+    width = d.shape[2]
+    fresh = out is None
+    inputs = [order, d, own_rest, own_high, recv_rest] + ([] if fresh else [out])
+    return call(
+        functools.partial(settle_kernel, chunk, fresh), inputs,
+        [IN_VMEM] * 5 + ([] if fresh else [IN_HBM]),
+        [jax.ShapeDtypeStruct((MICRO * BLOCK, width), jnp.bfloat16)], [IN_HBM],
+        scratch=[pltpu.VMEM((2 * BLOCK, width), jnp.bfloat16), pltpu.SemaphoreType.DMA((2,))],
+        flops=4 * BLOCK * 2 * BLOCK * width,
+        input_output_aliases={} if fresh else {5: 0},
+    )[0]
+
+
+def compact(hidden, exit_layer, lengths, kv_cache, norm_gain, w_qkv, w_out):
+    swap = [(i, i ^ 1) for i in range(4)]
+    up = [(0, 2), (1, 3)]
+    down = [(2, 0), (3, 1)]
+    features = w_qkv.shape[1]
+    query_width = w_out.shape[1]
+    context = kv_cache.shape[2]
+    tall = 2 * BLOCK
+    count = 4
+    lag = 3
+    exits = exit_layer.reshape(4, tall)
+    length_rows = lengths.reshape(4, tall)
+    total_width = float(2 * features)
+
+    def send(value, pairs):
+        return lax.ppermute(value, "section", pairs)
+
+    states = call(
+        split_kernel, [hidden[0]], [IN_HBM],
+        [pltpu.VMEM((tall, features), jnp.bfloat16)] * 2,
+        scratch=[pltpu.SemaphoreType.DMA((2,))],
+    )
+    moved = [send(states[i], down) for i in range(2)]
+    order, active, limits, fits = call(
+        prepare_kernel, [exits, length_rows], [IN_VMEM] * 2,
+        [
+            pltpu.VMEM((4, tall, tall), jnp.bfloat16),
+            pltpu.VMEM((4, tall, 128), jnp.float32),
+            pltpu.VMEM((2, 8, BLOCK // 2 * context), jnp.float32),
+            jax.ShapeDtypeStruct((1,), jnp.int32),
+        ],
+        [IN_VMEM] * 3 + [IN_SMEM],
+    )
+    arrived, low_rests, high_rests, settled, own_highs = [], [], [], [], []
+    for step in range(count + lag):
+        low, high = min(step, count - 1), max(step - lag, 0)
+        roles = "lower" if step < lag else "both" if step < count else "upper"
+        x = states[step] if step < 2 else moved[step - 2] if step < count else None
+        a = arrived[step - lag] if step >= lag else None
+        if step == 0:
+            keep, keep_sq, partial, held_proj = project(
+                roles, x, a, norm_gain, w_qkv[0], load="first"
+            )
+        elif step == 1:
+            keep, keep_sq, partial, held_out, held_cache = project(
+                roles, x, a, norm_gain, held_proj, "second", w_out[0], kv_cache[0]
+            )
+        else:
+            keep, keep_sq, partial = project(roles, x, a, norm_gain, held_proj)
+        if step == 0:
+            waiting = (keep, keep_sq, partial, x, a, roles, low, high)
+            continue
+        jobs = [(keep, keep_sq, partial, x, a, roles, low, high)]
+        if step == 1:
+            jobs = [waiting] + jobs
+        for keep, keep_sq, partial, x, a, roles, low, high in jobs:
+            received = send(partial, swap)
+            own = attend(roles, low, high, total_width, keep, keep_sq, received, held_cache, limits, order, query_width)
+            other = send(own, swap)
+            results = output(roles, low, high, own, other, active, order, x, a, held_out)
+            if roles != "upper":
+                arrived.append(send(results[0], up))
+                high_rests.append(send(results[1], up))
+                low_rests.append(results[2])
+            if roles != "lower":
+                settled.append(send(results[-2], down))
+                own_highs.append(results[-1])
+    out = None
+    for chunk in range(count):
+        out = settle(
+            chunk, order, settled[chunk], low_rests[chunk], own_highs[chunk], high_rests[chunk], out
+        )
+    return out, fits
+
+
+def paired_body(hidden, exit_layer, lengths, kv_cache, norm_gain, w_qkv, w_out):
+    arguments = (hidden, exit_layer, lengths, kv_cache, norm_gain, w_qkv, w_out)
+    out, fits = compact(*arguments)
+    return lax.cond(fits[0] > 0, lambda out, *rest: out, lambda out, *rest: body(*rest), out, *arguments)
+
+
 def solution(mesh):
+    paired = mesh.shape["section"] == 4
     return jax.shard_map(
-        body,
+        paired_body if paired else body,
         mesh=mesh,
         in_specs=(
             P("section", "blk", None),

time: 425 us -> 148 us (0.35)
  matrix products: 107 us -> 0 us
  waiting for transfers between devices: 143 us -> 61.9 us
  other arithmetic: 47.3 us -> 0 us
  loops' own time: 36.2 us -> 0.01 us
  Pallas kernels: 0 us -> 31.1 us
  local copies, waits for them, and re-layouts: 24.1 us -> 1.34 us
  starting transfers between devices: 64.2 us -> 52.2 us
    dot_general x40 -> x0, matrix products: 107 us -> none  [the longest x8 47.2 us: local_partials(): jnp.dot(scaled, proj_weight, preferred_element_type=jnp.float32)]
    ppermute x46 -> x28, waiting for transfers between devices: 143 us -> 61.9 us  [send(): return lax.ppermute(value, 'section', pairs)]
    another operation x28 -> x1, loops' own time: 36.2 us -> 0.01 us  [paired_body(): lax.cond(fits[0] > 0, lambda out, *rest: out, lambda out, *rest: body(*re...]
    pallas_call x0 -> x27, Pallas kernels: none -> 31.1 us  [call(): pl.pallas_call(kernel, in_specs=in_specs, out_specs=[IN_VMEM] * len(outs)...]
    dynamic_update_slice x9 -> x0, other arithmetic: 18.3 us -> none  [advance(): lax.dynamic_update_slice_in_dim(records, jnp.where(leaving[:, None], outg...]
    select_n x28 -> x0, other arithmetic: 14.5 us -> none  [the longest x9 11.7 us: advance(): relayed = jnp.where(on_turn & (segment_index > 0), own_block, arriving)]
    ppermute x46 -> x28, starting transfers between devices: 64.2 us -> 52.2 us  [send(): return lax.ppermute(value, 'section', pairs)]
    dynamic_slice x17 -> x0, local copies, waits for them, and re-layouts: 11.4 us -> none  [the longest x8 6.07 us: advance(): lax.dynamic_slice_in_dim(lengths, slot * BLOCK + shard_index * group_rows...]
  transfers between devices with their start and end apart: 46 -> 28, of which waited for: 27 -> 13; matrix products, arithmetic and copies ran while one was open for 21% -> 0% of each run, Pallas kernels for 0% -> 20%
where the time goes in v1:
time: 148 us
  waiting for transfers between devices  61.9 us (42%)
  starting transfers between devices  52.2 us (35%)
  Pallas kernels  31.1 us (21%)
    ppermute x28, waiting for transfers between devices, send(): return lax.ppermute(value, 'section', pairs)  61.9 us
    ppermute x28, starting transfers between devices, send(): return lax.ppermute(value, 'section', pairs)  52.2 us
    pallas_call x27, Pallas kernels, call(): pl.pallas_call(kernel, in_specs=in_specs, out_specs=[IN_VMEM] * len(outs)...  31.1 us
  transfers between devices with their start and end apart: 28, of which 13 were waited for; matrix products, arithmetic and copies ran while one was open for 0% of the time, Pallas kernels for 20%

profile of v1, /device:TPU:0, one launch (start us, length us, event | category | flops | bytes accessed | tf_op | source)
XLA Modules:
  0.0 147.7 jit_solution(6605161273473006112)
XLA Ops:
  0.0 1.6 %shard_map.76 = (bf16[128,4096]{1,0:T(8,128)(2,1)S(1)}, bf16[128,4096]{1,0:T(8,128)(2,1)S(1)}) custom-call(bf16[256,4096]{1,0:T(8,128)(2,1)} %bitcast.42), custom_call_target="tpu_custom_call" | custom-call | flops 100000000 | bytes 1000000 | tf_op jit(solution)/shard_map/pallas_call | solution.py:189
  2.9 4.9 %shard_map.77 = (f32[64,1280]{1,0:T(8,128)S(1)}, f32[64,128]{1,0:T(8,128)S(1)}, bf16[64,1408]{1,0:T(8,128)(2,1)S(1)}, bf16[4096,1280]{1,0:T(8,128)(2,1)S(1)}) custom-call(bf16[128,4096]{1,0:T(8,128)(2,1)S(1)} %get-tuple-element.516.refs_0_.refs_4_, bf16[1,4096]{1,0:T(2,128)(2,1)S(1)} %copy-done.5, bf16[4096,1280]{1,0:T(8,128)(2,1)} %bitcast.36), custom_call_target="tpu_custom_call" | custom-call | flops 1342177280 | bytes 1000000 | tf_op jit(solution)/shard_map/pallas_call | solution.py:189
  7.8 3.0 %collective-permute-start.7 = (bf16[64,1408]{1,0:T(8,128)(2,1)S(1)}, bf16[64,1408]{1,0:T(8,128)(2,1)S(1)}, u32[]{:S(2)}, u32[]{:S(2)}) collective-permute-start(bf16[64,1408]{1,0:T(8,128)(2,1)S(1)} %get-tuple-element.519), channel_id=1, source_target_pairs={{0,1},{1,0},{2,3},{3,2},{4,5},{5,4},{6,7},{7,6},{8,9},{9,8},{10,11... | collective-permute-start | bytes 540680 | tf_op jit(solution)/shard_map/ppermute | solution.py:741
  13.0 2.4 %shard_map.78 = (f32[64,1280]{1,0:T(8,128)S(1)}, f32[64,128]{1,0:T(8,128)S(1)}, bf16[64,1408]{1,0:T(8,128)(2,1)S(1)}, bf16[1024,4096]{1,0:T(8,128)(2,1)S(1)}, bf16[256,16,256]{2,1,0:T(8,128)(2,1)S(1)}) custom-call(bf16[128,4096]{1,0:T(8,128)(2,1)S(1)} %get-tuple-element.515.refs_0_.refs_4_, bf16[1,4096]{1,0:T(2,128)(2,1)S(1)} %copy-done.5, ...), custom_call_target="tpu_custom_call" | custom-call | flops 1342177280 | bytes 1000000 | tf_op jit(solution)/shard_map/pallas_call | solution.py:189
  16.2 1.7 %collective-permute-start.8 = (bf16[64,1024]{1,0:T(8,128)(2,1)S(1)}, bf16[64,1024]{1,0:T(8,128)(2,1)S(1)}, u32[]{:S(2)}, u32[]{:S(2)}) collective-permute-start(bf16[64,1024]{1,0:T(8,128)(2,1)S(1)} %shard_map.79.refs_0_), channel_id=1, source_target_pairs={{0,1},{1,0},{2,3},{3,2},{4,5},{5,4},{6,7},{7,6},{8,9},{9,8},{10,11... | collective-permute-start | bytes 393224 | tf_op jit(solution)/shard_map/ppermute | solution.py:741
  17.9 3.3 %collective-permute-done.8.refs_1_ = bf16[64,1024]{1,0:T(8,128)(2,1)S(1)} collective-permute-done((bf16[64,1024]{1,0:T(8,128)(2,1)S(1)}, bf16[64,1024]{1,0:T(8,128)(2,1)S(1)}, u32[]{:S(2)}, u32[]{:S(2)}) %collective-permute-start.8) | collective-permute-done | bytes 131104 | tf_op jit(solution)/shard_map/ppermute | solution.py:741
  21.2 3.2 %shard_map.80 = (bf16[2,40,4096]{2,1,0:T(8,128)(2,1)S(1)}, bf16[2,24,2048]{2,1,0:T(8,128)(2,1)S(1)}, bf16[2,24,2048]{2,1,0:T(8,128)(2,1)S(1)}) custom-call(bf16[64,1024]{1,0:T(8,128)(2,1)S(1)} %shard_map.79.refs_0_, bf16[64,1024]{1,0:T(8,128)(2,1)S(1)} %collective-permute-done.8.refs_1_, f32[4,128,128]{2,1,0:T(8,128)S(1)} %get-tuple-element.523.refs_2_, ...), custom_call_target="tpu_custom_call" | custom-call | flops 1073741824 | bytes 1000000 | tf_op jit(solution)/shard_map/pallas_call | solution.py:189
  25.8 1.7 %collective-permute-start.25 = (bf16[64,1408]{1,0:T(8,128)(2,1)S(1)}, bf16[64,1408]{1,0:T(8,128)(2,1)S(1)}, u32[]{:S(2)}, u32[]{:S(2)}) collective-permute-start(bf16[64,1408]{1,0:T(8,128)(2,1)S(1)} %get-tuple-element.550), channel_id=1, source_target_pairs={{0,1},{1,0},{2,3},{3,2},{4,5},{5,4},{6,7},{7,6},{8,9},{9,8},{10,11... | collective-permute-start | bytes 540680 | tf_op jit(solution)/shard_map/ppermute | solution.py:741
  27.5 2.3 %collective-permute-done.17.refs_0_.refs_4_ = bf16[128,4096]{1,0:T(8,128)(2,1)S(1)} collective-permute-done((bf16[128,4096]{1,0:T(8,128)(2,1)S(1)}, bf16[128,4096]{1,0:T(8,128)(2,1)S(1)}, u32[]{:S(2)}, u32[]{:S(2)}) %collective-permute-start.17) | collective-permute-done | bytes 1048608 | tf_op jit(solution)/shard_map/ppermute | solution.py:741
  29.9 1.7 %shard_map.87 = (f32[64,1280]{1,0:T(8,128)S(1)}, f32[64,128]{1,0:T(8,128)S(1)}, bf16[64,1408]{1,0:T(8,128)(2,1)S(1)}) custom-call(bf16[128,4096]{1,0:T(8,128)(2,1)S(1)} %collective-permute-done.17.refs_0_.refs_4_, bf16[1,4096]{1,0:T(2,128)(2,1)S(1)} %copy-done.5, bf16[4096,1280]{1,0:T(8,128)(2,1)S(1)} %get-tuple-element.520.refs_2_.refs_3_), custom_call_target="tpu_custom_call" | custom-call | flops 1342177280 | bytes 1000000 | tf_op jit(solution)/shard_map/pallas_call | solution.py:189
  31.6 2.7 %collective-permute-start.18 = (bf16[64,1408]{1,0:T(8,128)(2,1)S(1)}, bf16[64,1408]{1,0:T(8,128)(2,1)S(1)}, u32[]{:S(2)}, u32[]{:S(2)}) collective-permute-start(bf16[64,1408]{1,0:T(8,128)(2,1)S(1)} %get-tuple-element.539), channel_id=1, source_target_pairs={{0,1},{1,0},{2,3},{3,2},{4,5},{5,4},{6,7},{7,6},{8,9},{9,8},{10,11... | collective-permute-start | bytes 540680 | tf_op jit(solution)/shard_map/ppermute | solution.py:741
  35.0 3.8 %collective-permute-done.9.refs_1_.refs_5_ = bf16[2,40,4096]{2,1,0:T(8,128)(2,1)S(1)} collective-permute-done((bf16[2,40,4096]{2,1,0:T(8,128)(2,1)S(1)}, bf16[2,40,4096]{2,1,0:T(8,128)(2,1)S(1)}, u32[]{:S(2)}, u32[]{:S(2)}) %collective-permute-start.9) | collective-permute-done | bytes 655392 | tf_op jit(solution)/shard_map/ppermute | solution.py:741
  38.9 12.6 %collective-permute-done.6.refs_0_.refs_4_ = bf16[128,4096]{1,0:T(8,128)(2,1)S(1)} collective-permute-done((bf16[128,4096]{1,0:T(8,128)(2,1)S(1)}, bf16[128,4096]{1,0:T(8,128)(2,1)S(1)}, u32[]{:S(2)}, u32[]{:S(2)}) %collective-permute-start.6) | collective-permute-done | bytes 1048608 | tf_op jit(solution)/shard_map/ppermute | solution.py:741
  51.5 1.9 %shard_map.81 = (f32[64,1280]{1,0:T(8,128)S(1)}, f32[64,128]{1,0:T(8,128)S(1)}, bf16[64,1408]{1,0:T(8,128)(2,1)S(1)}) custom-call(bf16[128,4096]{1,0:T(8,128)(2,1)S(1)} %collective-permute-done.6.refs_0_.refs_4_, bf16[2,40,4096]{2,1,0:T(8,128)(2,1)S(1)} %collective-permute-done.9.refs_1_.refs_5_, bf16[1,4096]{1,0:T(2,128)(2,1)S(1)} %copy-done.5, ...), custom_call_target="tpu_custom_call" | custom-call | flops 1342177280 | bytes 1000000 | tf_op jit(solution)/shard_map/pallas_call | solution.py:189
  53.4 2.4 %collective-permute-start.10 = (bf16[64,1408]{1,0:T(8,128)(2,1)S(1)}, bf16[64,1408]{1,0:T(8,128)(2,1)S(1)}, u32[]{:S(2)}, u32[]{:S(2)}) collective-permute-start(bf16[64,1408]{1,0:T(8,128)(2,1)S(1)} %get-tuple-element.528), channel_id=1, source_target_pairs={{0,1},{1,0},{2,3},{3,2},{4,5},{5,4},{6,7},{7,6},{8,9},{9,8},{10,11... | collective-permute-start | bytes 540680 | tf_op jit(solution)/shard_map/ppermute | solution.py:741
  56.6 3.2 %shard_map.94 = (bf16[2,40,4096]{2,1,0:T(8,128)(2,1)S(1)}, bf16[2,24,2048]{2,1,0:T(8,128)(2,1)S(1)}, bf16[2,24,2048]{2,1,0:T(8,128)(2,1)S(1)}) custom-call(bf16[64,1024]{1,0:T(8,128)(2,1)S(1)} %shard_map.93.refs_0_, bf16[64,1024]{1,0:T(8,128)(2,1)S(1)} %collective-permute-done.26.refs_1_, f32[4,128,128]{2,1,0:T(8,128)S(1)} %get-tuple-element.523.refs_2_, ...), custom_call_target="tpu_custom_call" | custom-call | flops 1073741824 | bytes 1000000 | tf_op jit(solution)/shard_map/pallas_call | solution.py:189
  62.1 2.1 %collective-permute-start.11 = (bf16[64,1024]{1,0:T(8,128)(2,1)S(1)}, bf16[64,1024]{1,0:T(8,128)(2,1)S(1)}, u32[]{:S(2)}, u32[]{:S(2)}) collective-permute-start(bf16[64,1024]{1,0:T(8,128)(2,1)S(1)} %shard_map.82.refs_0_), channel_id=1, source_target_pairs={{0,1},{1,0},{2,3},{3,2},{4,5},{5,4},{6,7},{7,6},{8,9},{9,8},{10,11... | collective-permute-start | bytes 393224 | tf_op jit(solution)/shard_map/ppermute | solution.py:741
  64.2 3.2 %shard_map.89 = (bf16[2,40,4096]{2,1,0:T(8,128)(2,1)S(1)}, bf16[2,24,2048]{2,1,0:T(8,128)(2,1)S(1)}, bf16[2,24,2048]{2,1,0:T(8,128)(2,1)S(1)}) custom-call(bf16[64,1024]{1,0:T(8,128)(2,1)S(1)} %shard_map.88.refs_0_, bf16[64,1024]{1,0:T(8,128)(2,1)S(1)} %collective-permute-done.19.refs_1_, f32[4,128,128]{2,1,0:T(8,128)S(1)} %get-tuple-element.523.refs_2_, ...), custom_call_target="tpu_custom_call" | custom-call | flops 1073741824 | bytes 1000000 | tf_op jit(solution)/shard_map/pallas_call | solution.py:189
  68.7 3.2 %shard_map.83 = (bf16[2,40,4096]{2,1,0:T(8,128)(2,1)S(1)}, bf16[2,24,2048]{2,1,0:T(8,128)(2,1)S(1)}, bf16[2,24,2048]{2,1,0:T(8,128)(2,1)S(1)}, bf16[2,40,2048]{2,1,0:T(8,128)(2,1)S(1)}, bf16[2,40,2048]{2,1,0:T(8,128)(2,1)S(1)}) custom-call(bf16[64,1024]{1,0:T(8,128)(2,1)S(1)} %shard_map.82.refs_0_, bf16[64,1024]{1,0:T(8,128)(2,1)S(1)} %collective-permute-done.11.refs_1_, ...), custom_call_target="tpu_custom_call" | custom-call | flops 1073741824 | bytes 1000000 | tf_op jit(solution)/shard_map/pallas_call | solution.py:189
  73.3 2.9 %collective-permute-done.27.refs_0_.refs_4_ = bf16[2,40,4096]{2,1,0:T(8,128)(2,1)S(1)} collective-permute-done((bf16[2,40,4096]{2,1,0:T(8,128)(2,1)S(1)}, bf16[2,40,4096]{2,1,0:T(8,128)(2,1)S(1)}, u32[]{:S(2)}, u32[]{:S(2)}) %collective-permute-start.27) | collective-permute-done | bytes 655392 | tf_op jit(solution)/shard_map/ppermute | solution.py:741
  76.2 2.0 %collective-permute-start.28 = (bf16[64,1408]{1,0:T(8,128)(2,1)S(1)}, bf16[64,1408]{1,0:T(8,128)(2,1)S(1)}, u32[]{:S(2)}, u32[]{:S(2)}) collective-permute-start(bf16[64,1408]{1,0:T(8,128)(2,1)S(1)} %get-tuple-element.554), channel_id=1, source_target_pairs={{0,1},{1,0},{2,3},{3,2},{4,5},{5,4},{6,7},{7,6},{8,9},{9,8},{10,11... | collective-permute-start | bytes 540680 | tf_op jit(solution)/shard_map/ppermute | solution.py:741
  78.2 12.1 %collective-permute-done.20.refs_0_.refs_4_ = bf16[2,40,4096]{2,1,0:T(8,128)(2,1)S(1)} collective-permute-done((bf16[2,40,4096]{2,1,0:T(8,128)(2,1)S(1)}, bf16[2,40,4096]{2,1,0:T(8,128)(2,1)S(1)}, u32[]{:S(2)}, u32[]{:S(2)}) %collective-permute-start.20) | collective-permute-done | bytes 655392 | tf_op jit(solution)/shard_map/ppermute | solution.py:741
  90.3 2.0 %collective-permute-start.21 = (bf16[64,1408]{1,0:T(8,128)(2,1)S(1)}, bf16[64,1408]{1,0:T(8,128)(2,1)S(1)}, u32[]{:S(2)}, u32[]{:S(2)}) collective-permute-start(bf16[64,1408]{1,0:T(8,128)(2,1)S(1)} %get-tuple-element.543), channel_id=1, source_target_pairs={{0,1},{1,0},{2,3},{3,2},{4,5},{5,4},{6,7},{7,6},{8,9},{9,8},{10,11... | collective-permute-start | bytes 540680 | tf_op jit(solution)/shard_map/ppermute | solution.py:741
  92.2 10.1 %collective-permute-done.12.refs_0_.refs_4_ = bf16[2,40,4096]{2,1,0:T(8,128)(2,1)S(1)} collective-permute-done((bf16[2,40,4096]{2,1,0:T(8,128)(2,1)S(1)}, bf16[2,40,4096]{2,1,0:T(8,128)(2,1)S(1)}, u32[]{:S(2)}, u32[]{:S(2)}) %collective-permute-start.12) | collective-permute-done | bytes 655392 | tf_op jit(solution)/shard_map/ppermute | solution.py:741
  102.3 1.7 %collective-permute-start.13 = (bf16[64,1408]{1,0:T(8,128)(2,1)S(1)}, bf16[64,1408]{1,0:T(8,128)(2,1)S(1)}, u32[]{:S(2)}, u32[]{:S(2)}) collective-permute-start(bf16[64,1408]{1,0:T(8,128)(2,1)S(1)} %get-tuple-element.532), channel_id=1, source_target_pairs={{0,1},{1,0},{2,3},{3,2},{4,5},{5,4},{6,7},{7,6},{8,9},{9,8},{10,11... | collective-permute-start | bytes 540680 | tf_op jit(solution)/shard_map/ppermute | solution.py:741
  104.0 6.1 %collective-permute-start.31 = (bf16[2,24,2048]{2,1,0:T(8,128)(2,1)S(1)}, bf16[2,24,2048]{2,1,0:T(8,128)(2,1)S(1)}, u32[]{:S(2)}, u32[]{:S(2)}) collective-permute-start(bf16[2,24,2048]{2,1,0:T(8,128)(2,1)S(1)} %get-tuple-element.558), channel_id=1, source_target_pairs={{0,2},{1,3},{4,6},{5,7},{8,10},{9,11},{12,14},{13,15},{16,18},{17,... | collective-permute-start | bytes 589832 | tf_op jit(solution)/shard_map/ppermute | solution.py:741
  111.9 1.7 %collective-permute-start.22 = (bf16[64,1024]{1,0:T(8,128)(2,1)S(1)}, bf16[64,1024]{1,0:T(8,128)(2,1)S(1)}, u32[]{:S(2)}, u32[]{:S(2)}) collective-permute-start(bf16[64,1024]{1,0:T(8,128)(2,1)S(1)} %shard_map.91.refs_0_), channel_id=1, source_target_pairs={{0,1},{1,0},{2,3},{3,2},{4,5},{5,4},{6,7},{7,6},{8,9},{9,8},{10,11... | collective-permute-start | bytes 393224 | tf_op jit(solution)/shard_map/ppermute | solution.py:741
  113.9 3.1 %collective-permute-done.29.refs_1_ = bf16[64,1024]{1,0:T(8,128)(2,1)S(1)} collective-permute-done((bf16[64,1024]{1,0:T(8,128)(2,1)S(1)}, bf16[64,1024]{1,0:T(8,128)(2,1)S(1)}, u32[]{:S(2)}, u32[]{:S(2)}) %collective-permute-start.29) | collective-permute-done | bytes 131104 | tf_op jit(solution)/shard_map/ppermute | solution.py:741
  122.5 8.5 %collective-permute-start.24 = (bf16[2,24,2048]{2,1,0:T(8,128)(2,1)S(1)}, bf16[2,24,2048]{2,1,0:T(8,128)(2,1)S(1)}, u32[]{:S(2)}, u32[]{:S(2)}) collective-permute-start(bf16[2,24,2048]{2,1,0:T(8,128)(2,1)S(1)} %get-tuple-element.547), channel_id=1, source_target_pairs={{0,2},{1,3},{4,6},{5,7},{8,10},{9,11},{12,14},{13,15},{16,18},{17,... | collective-permute-start | bytes 589832 | tf_op jit(solution)/shard_map/ppermute | solution.py:741
  131.0 5.7 %collective-permute-done.32.refs_1_ = bf16[2,40,2048]{2,1,0:T(8,128)(2,1)S(1)} collective-permute-done((bf16[2,40,2048]{2,1,0:T(8,128)(2,1)S(1)}, bf16[2,40,2048]{2,1,0:T(8,128)(2,1)S(1)}, u32[]{:S(2)}, u32[]{:S(2)}) %collective-permute-start.32) | collective-permute-done | bytes 327712 | tf_op jit(solution)/shard_map/ppermute | solution.py:741
  139.9 2.6 %collective-permute-done.23.refs_1_ = bf16[2,40,2048]{2,1,0:T(8,128)(2,1)S(1)} collective-permute-done((bf16[2,40,2048]{2,1,0:T(8,128)(2,1)S(1)}, bf16[2,40,2048]{2,1,0:T(8,128)(2,1)S(1)}, u32[]{:S(2)}, u32[]{:S(2)}) %collective-permute-start.23) | collective-permute-done | bytes 327712 | tf_op jit(solution)/shard_map/ppermute | solution.py:741
  142.8 3.1 %collective-permute-done.15.refs_1_ = bf16[2,40,2048]{2,1,0:T(8,128)(2,1)S(1)} collective-permute-done((bf16[2,40,2048]{2,1,0:T(8,128)(2,1)S(1)}, bf16[2,40,2048]{2,1,0:T(8,128)(2,1)S(1)}, u32[]{:S(2)}, u32[]{:S(2)}) %collective-permute-start.15) | collective-permute-done | bytes 327712 | tf_op jit(solution)/shard_map/ppermute | solution.py:741
  (64 shorter events, 24.0 us)
Async XLA Ops:
  1.6 28.3 %collective-permute-start.17 = (bf16[128,4096]{1,0:T(8,128)(2,1)S(1)}, bf16[128,4096]{1,0:T(8,128)(2,1)S(1)}, u32[]{:S(2)}, u32[]{:S(2)}) collective-permute-start(bf16[128,4096]{1,0:T(8,128)(2,1)S(1)} %get-tuple-element.516.refs_0_.refs_4_), channel_id=1, source_target_pairs={{2,0},{3,1},{6,4},{7,5},{10,8},{11,9},{14,12},{15,13},{18,16},{19,... | collective-permute-start | bytes 3145736 | tf_op jit(solution)/shard_map/ppermute | solution.py:741
  2.9 9.3 %copy-start.6 = (s32[512]{0:T(512)S(1)}, s32[512]{0:T(512)}, u32[]{:S(2)}) copy-start(s32[512]{0:T(512)} %param.18) | copy-start | bytes 6148
  2.9 9.3 %copy-start.7 = (s32[512]{0:T(512)S(1)}, s32[512]{0:T(512)}, u32[]{:S(2)}) copy-start(s32[512]{0:T(512)} %param.19) | copy-start | bytes 6148
  2.9 10.1 %copy-start = (bf16[1,1024,4096]{2,1,0:T(8,128)(2,1)S(1)}, bf16[1,1024,4096]{2,1,0:T(8,128)(2,1)}, u32[]{:S(2)}) copy-start(bf16[1,1024,4096]{2,1,0:T(8,128)(2,1)} %param.23) | copy-start | bytes 25165828
  2.9 10.1 %copy-start.3 = (bf16[1,256,16,256]{3,2,1,0:T(8,128)(2,1)S(1)}, bf16[1,256,16,256]{3,2,1,0:T(8,128)(2,1)}, u32[]{:S(2)}) copy-start(bf16[1,256,16,256]{3,2,1,0:T(8,128)(2,1)} %param.20) | copy-start | bytes 6291460
  7.8 7.6 %collective-permute-start.7 = (bf16[64,1408]{1,0:T(8,128)(2,1)S(1)}, bf16[64,1408]{1,0:T(8,128)(2,1)S(1)}, u32[]{:S(2)}, u32[]{:S(2)}) collective-permute-start(bf16[64,1408]{1,0:T(8,128)(2,1)S(1)} %get-tuple-element.519), channel_id=1, source_target_pairs={{0,1},{1,0},{2,3},{3,2},{4,5},{5,4},{6,7},{7,6},{8,9},{9,8},{10,11... | collective-permute-start | bytes 540680 | tf_op jit(solution)/shard_map/ppermute | solution.py:741
  10.9 40.6 %collective-permute-start.6 = (bf16[128,4096]{1,0:T(8,128)(2,1)S(1)}, bf16[128,4096]{1,0:T(8,128)(2,1)S(1)}, u32[]{:S(2)}, u32[]{:S(2)}) collective-permute-start(bf16[128,4096]{1,0:T(8,128)(2,1)S(1)} %get-tuple-element.515.refs_0_.refs_4_), channel_id=1, source_target_pairs={{2,0},{3,1},{6,4},{7,5},{10,8},{11,9},{14,12},{15,13},{18,16},{19,... | collective-permute-start | bytes 3145736 | tf_op jit(solution)/shard_map/ppermute | solution.py:741
  16.2 5.0 %collective-permute-start.8 = (bf16[64,1024]{1,0:T(8,128)(2,1)S(1)}, bf16[64,1024]{1,0:T(8,128)(2,1)S(1)}, u32[]{:S(2)}, u32[]{:S(2)}) collective-permute-start(bf16[64,1024]{1,0:T(8,128)(2,1)S(1)} %shard_map.79.refs_0_), channel_id=1, source_target_pairs={{0,1},{1,0},{2,3},{3,2},{4,5},{5,4},{6,7},{7,6},{8,9},{9,8},{10,11... | collective-permute-start | bytes 393224 | tf_op jit(solution)/shard_map/ppermute | solution.py:741
  24.5 14.4 %collective-permute-start.9 = (bf16[2,40,4096]{2,1,0:T(8,128)(2,1)S(1)}, bf16[2,40,4096]{2,1,0:T(8,128)(2,1)S(1)}, u32[]{:S(2)}, u32[]{:S(2)}) collective-permute-start(bf16[2,40,4096]{2,1,0:T(8,128)(2,1)S(1)} %get-tuple-element.525), channel_id=1, source_target_pairs={{0,2},{1,3},{4,6},{5,7},{8,10},{9,11},{12,14},{13,15},{16,18},{17,... | collective-permute-start | bytes 1966088 | tf_op jit(solution)/shard_map/ppermute | solution.py:741
  25.8 8.4 %collective-permute-start.25 = (bf16[64,1408]{1,0:T(8,128)(2,1)S(1)}, bf16[64,1408]{1,0:T(8,128)(2,1)S(1)}, u32[]{:S(2)}, u32[]{:S(2)}) collective-permute-start(bf16[64,1408]{1,0:T(8,128)(2,1)S(1)} %get-tuple-element.550), channel_id=1, source_target_pairs={{0,1},{1,0},{2,3},{3,2},{4,5},{5,4},{6,7},{7,6},{8,9},{9,8},{10,11... | collective-permute-start | bytes 540680 | tf_op jit(solution)/shard_map/ppermute | solution.py:741
  31.6 24.2 %collective-permute-start.18 = (bf16[64,1408]{1,0:T(8,128)(2,1)S(1)}, bf16[64,1408]{1,0:T(8,128)(2,1)S(1)}, u32[]{:S(2)}, u32[]{:S(2)}) collective-permute-start(bf16[64,1408]{1,0:T(8,128)(2,1)S(1)} %get-tuple-element.539), channel_id=1, source_target_pairs={{0,1},{1,0},{2,3},{3,2},{4,5},{5,4},{6,7},{7,6},{8,9},{9,8},{10,11... | collective-permute-start | bytes 540680 | tf_op jit(solution)/shard_map/ppermute | solution.py:741
  34.9 21.7 %collective-permute-start.26 = (bf16[64,1024]{1,0:T(8,128)(2,1)S(1)}, bf16[64,1024]{1,0:T(8,128)(2,1)S(1)}, u32[]{:S(2)}, u32[]{:S(2)}) collective-permute-start(bf16[64,1024]{1,0:T(8,128)(2,1)S(1)} %shard_map.93.refs_0_), channel_id=1, source_target_pairs={{0,1},{1,0},{2,3},{3,2},{4,5},{5,4},{6,7},{7,6},{8,9},{9,8},{10,11... | collective-permute-start | bytes 393224 | tf_op jit(solution)/shard_map/ppermute | solution.py:741
  53.4 7.7 %collective-permute-start.10 = (bf16[64,1408]{1,0:T(8,128)(2,1)S(1)}, bf16[64,1408]{1,0:T(8,128)(2,1)S(1)}, u32[]{:S(2)}, u32[]{:S(2)}) collective-permute-start(bf16[64,1408]{1,0:T(8,128)(2,1)S(1)} %get-tuple-element.528), channel_id=1, source_target_pairs={{0,1},{1,0},{2,3},{3,2},{4,5},{5,4},{6,7},{7,6},{8,9},{9,8},{10,11... | collective-permute-start | bytes 540680 | tf_op jit(solution)/shard_map/ppermute | solution.py:741
  56.5 7.7 %collective-permute-start.19 = (bf16[64,1024]{1,0:T(8,128)(2,1)S(1)}, bf16[64,1024]{1,0:T(8,128)(2,1)S(1)}, u32[]{:S(2)}, u32[]{:S(2)}) collective-permute-start(bf16[64,1024]{1,0:T(8,128)(2,1)S(1)} %shard_map.88.refs_0_), channel_id=1, source_target_pairs={{0,1},{1,0},{2,3},{3,2},{4,5},{5,4},{6,7},{7,6},{8,9},{9,8},{10,11... | collective-permute-start | bytes 393224 | tf_op jit(solution)/shard_map/ppermute | solution.py:741
  59.8 16.4 %collective-permute-start.27 = (bf16[2,40,4096]{2,1,0:T(8,128)(2,1)S(1)}, bf16[2,40,4096]{2,1,0:T(8,128)(2,1)S(1)}, u32[]{:S(2)}, u32[]{:S(2)}) collective-permute-start(bf16[2,40,4096]{2,1,0:T(8,128)(2,1)S(1)} %get-tuple-element.551), channel_id=1, source_target_pairs={{0,2},{1,3},{4,6},{5,7},{8,10},{9,11},{12,14},{13,15},{16,18},{17,... | collective-permute-start | bytes 1966088 | tf_op jit(solution)/shard_map/ppermute | solution.py:741
  62.1 6.6 %collective-permute-start.11 = (bf16[64,1024]{1,0:T(8,128)(2,1)S(1)}, bf16[64,1024]{1,0:T(8,128)(2,1)S(1)}, u32[]{:S(2)}, u32[]{:S(2)}) collective-permute-start(bf16[64,1024]{1,0:T(8,128)(2,1)S(1)} %shard_map.82.refs_0_), channel_id=1, source_target_pairs={{0,1},{1,0},{2,3},{3,2},{4,5},{5,4},{6,7},{7,6},{8,9},{9,8},{10,11... | collective-permute-start | bytes 393224 | tf_op jit(solution)/shard_map/ppermute | solution.py:741
  67.4 22.9 %collective-permute-start.20 = (bf16[2,40,4096]{2,1,0:T(8,128)(2,1)S(1)}, bf16[2,40,4096]{2,1,0:T(8,128)(2,1)S(1)}, u32[]{:S(2)}, u32[]{:S(2)}) collective-permute-start(bf16[2,40,4096]{2,1,0:T(8,128)(2,1)S(1)} %get-tuple-element.540), channel_id=1, source_target_pairs={{0,2},{1,3},{4,6},{5,7},{8,10},{9,11},{12,14},{13,15},{16,18},{17,... | collective-permute-start | bytes 1966088 | tf_op jit(solution)/shard_map/ppermute | solution.py:741
  72.0 30.3 %collective-permute-start.12 = (bf16[2,40,4096]{2,1,0:T(8,128)(2,1)S(1)}, bf16[2,40,4096]{2,1,0:T(8,128)(2,1)S(1)}, u32[]{:S(2)}, u32[]{:S(2)}) collective-permute-start(bf16[2,40,4096]{2,1,0:T(8,128)(2,1)S(1)} %get-tuple-element.529), channel_id=1, source_target_pairs={{0,2},{1,3},{4,6},{5,7},{8,10},{9,11},{12,14},{13,15},{16,18},{17,... | collective-permute-start | bytes 1966088 | tf_op jit(solution)/shard_map/ppermute | solution.py:741
  76.2 35.2 %collective-permute-start.28 = (bf16[64,1408]{1,0:T(8,128)(2,1)S(1)}, bf16[64,1408]{1,0:T(8,128)(2,1)S(1)}, u32[]{:S(2)}, u32[]{:S(2)}) collective-permute-start(bf16[64,1408]{1,0:T(8,128)(2,1)S(1)} %get-tuple-element.554), channel_id=1, source_target_pairs={{0,1},{1,0},{2,3},{3,2},{4,5},{5,4},{6,7},{7,6},{8,9},{9,8},{10,11... | collective-permute-start | bytes 540680 | tf_op jit(solution)/shard_map/ppermute | solution.py:741
  90.3 21.6 %collective-permute-start.21 = (bf16[64,1408]{1,0:T(8,128)(2,1)S(1)}, bf16[64,1408]{1,0:T(8,128)(2,1)S(1)}, u32[]{:S(2)}, u32[]{:S(2)}) collective-permute-start(bf16[64,1408]{1,0:T(8,128)(2,1)S(1)} %get-tuple-element.543), channel_id=1, source_target_pairs={{0,1},{1,0},{2,3},{3,2},{4,5},{5,4},{6,7},{7,6},{8,9},{9,8},{10,11... | collective-permute-start | bytes 540680 | tf_op jit(solution)/shard_map/ppermute | solution.py:741
  102.3 11.3 %collective-permute-start.13 = (bf16[64,1408]{1,0:T(8,128)(2,1)S(1)}, bf16[64,1408]{1,0:T(8,128)(2,1)S(1)}, u32[]{:S(2)}, u32[]{:S(2)}) collective-permute-start(bf16[64,1408]{1,0:T(8,128)(2,1)S(1)} %get-tuple-element.532), channel_id=1, source_target_pairs={{0,1},{1,0},{2,3},{3,2},{4,5},{5,4},{6,7},{7,6},{8,9},{9,8},{10,11... | collective-permute-start | bytes 540680 | tf_op jit(solution)/shard_map/ppermute | solution.py:741
  104.0 17.2 %collective-permute-start.31 = (bf16[2,24,2048]{2,1,0:T(8,128)(2,1)S(1)}, bf16[2,24,2048]{2,1,0:T(8,128)(2,1)S(1)}, u32[]{:S(2)}, u32[]{:S(2)}) collective-permute-start(bf16[2,24,2048]{2,1,0:T(8,128)(2,1)S(1)} %get-tuple-element.558), channel_id=1, source_target_pairs={{0,2},{1,3},{4,6},{5,7},{8,10},{9,11},{12,14},{13,15},{16,18},{17,... | collective-permute-start | bytes 589832 | tf_op jit(solution)/shard_map/ppermute | solution.py:741
  110.1 12.4 %collective-permute-start.33 = (bf16[2,24,2048]{2,1,0:T(8,128)(2,1)S(1)}, bf16[2,24,2048]{2,1,0:T(8,128)(2,1)S(1)}, u32[]{:S(2)}, u32[]{:S(2)}) collective-permute-start(bf16[2,24,2048]{2,1,0:T(8,128)(2,1)S(1)} %get-tuple-element.562), channel_id=1, source_target_pairs={{0,2},{1,3},{4,6},{5,7},{8,10},{9,11},{12,14},{13,15},{16,18},{17,... | collective-permute-start | bytes 589832 | tf_op jit(solution)/shard_map/ppermute | solution.py:741
  111.5 5.6 %collective-permute-start.29 = (bf16[64,1024]{1,0:T(8,128)(2,1)S(1)}, bf16[64,1024]{1,0:T(8,128)(2,1)S(1)}, u32[]{:S(2)}, u32[]{:S(2)}) collective-permute-start(bf16[64,1024]{1,0:T(8,128)(2,1)S(1)} %shard_map.96.refs_0_), channel_id=1, source_target_pairs={{0,1},{1,0},{2,3},{3,2},{4,5},{5,4},{6,7},{7,6},{8,9},{9,8},{10,11... | collective-permute-start | bytes 393224 | tf_op jit(solution)/shard_map/ppermute | solution.py:741
  111.9 6.6 %collective-permute-start.22 = (bf16[64,1024]{1,0:T(8,128)(2,1)S(1)}, bf16[64,1024]{1,0:T(8,128)(2,1)S(1)}, u32[]{:S(2)}, u32[]{:S(2)}) collective-permute-start(bf16[64,1024]{1,0:T(8,128)(2,1)S(1)} %shard_map.91.refs_0_), channel_id=1, source_target_pairs={{0,1},{1,0},{2,3},{3,2},{4,5},{5,4},{6,7},{7,6},{8,9},{9,8},{10,11... | collective-permute-start | bytes 393224 | tf_op jit(solution)/shard_map/ppermute | solution.py:741
  113.6 6.3 %collective-permute-start.14 = (bf16[64,1024]{1,0:T(8,128)(2,1)S(1)}, bf16[64,1024]{1,0:T(8,128)(2,1)S(1)}, u32[]{:S(2)}, u32[]{:S(2)}) collective-permute-start(bf16[64,1024]{1,0:T(8,128)(2,1)S(1)} %shard_map.85.refs_0_), channel_id=1, source_target_pairs={{0,1},{1,0},{2,3},{3,2},{4,5},{5,4},{6,7},{7,6},{8,9},{9,8},{10,11... | collective-permute-start | bytes 393224 | tf_op jit(solution)/shard_map/ppermute | solution.py:741
  117.1 22.2 %collective-permute-start.30 = (bf16[2,40,2048]{2,1,0:T(8,128)(2,1)S(1)}, bf16[2,40,2048]{2,1,0:T(8,128)(2,1)S(1)}, u32[]{:S(2)}, u32[]{:S(2)}) collective-permute-start(bf16[2,40,2048]{2,1,0:T(8,128)(2,1)S(1)} %get-tuple-element.555), channel_id=1, source_target_pairs={{2,0},{3,1},{6,4},{7,5},{10,8},{11,9},{14,12},{15,13},{18,16},{19,... | collective-permute-start | bytes 983048 | tf_op jit(solution)/shard_map/ppermute | solution.py:741
  118.5 18.3 %collective-permute-start.32 = (bf16[2,40,2048]{2,1,0:T(8,128)(2,1)S(1)}, bf16[2,40,2048]{2,1,0:T(8,128)(2,1)S(1)}, u32[]{:S(2)}, u32[]{:S(2)}) collective-permute-start(bf16[2,40,2048]{2,1,0:T(8,128)(2,1)S(1)} %get-tuple-element.559), channel_id=1, source_target_pairs={{2,0},{3,1},{6,4},{7,5},{10,8},{11,9},{14,12},{15,13},{18,16},{19,... | collective-permute-start | bytes 983048 | tf_op jit(solution)/shard_map/ppermute | solution.py:741
  119.9 22.6 %collective-permute-start.23 = (bf16[2,40,2048]{2,1,0:T(8,128)(2,1)S(1)}, bf16[2,40,2048]{2,1,0:T(8,128)(2,1)S(1)}, u32[]{:S(2)}, u32[]{:S(2)}) collective-permute-start(bf16[2,40,2048]{2,1,0:T(8,128)(2,1)S(1)} %get-tuple-element.544), channel_id=1, source_target_pairs={{2,0},{3,1},{6,4},{7,5},{10,8},{11,9},{14,12},{15,13},{18,16},{19,... | collective-permute-start | bytes 983048 | tf_op jit(solution)/shard_map/ppermute | solution.py:741
  121.2 24.8 %collective-permute-start.15 = (bf16[2,40,2048]{2,1,0:T(8,128)(2,1)S(1)}, bf16[2,40,2048]{2,1,0:T(8,128)(2,1)S(1)}, u32[]{:S(2)}, u32[]{:S(2)}) collective-permute-start(bf16[2,40,2048]{2,1,0:T(8,128)(2,1)S(1)} %get-tuple-element.533), channel_id=1, source_target_pairs={{2,0},{3,1},{6,4},{7,5},{10,8},{11,9},{14,12},{15,13},{18,16},{19,... | collective-permute-start | bytes 983048 | tf_op jit(solution)/shard_map/ppermute | solution.py:741
  122.5 17.4 %collective-permute-start.24 = (bf16[2,24,2048]{2,1,0:T(8,128)(2,1)S(1)}, bf16[2,24,2048]{2,1,0:T(8,128)(2,1)S(1)}, u32[]{:S(2)}, u32[]{:S(2)}) collective-permute-start(bf16[2,24,2048]{2,1,0:T(8,128)(2,1)S(1)} %get-tuple-element.547), channel_id=1, source_target_pairs={{0,2},{1,3},{4,6},{5,7},{8,10},{9,11},{12,14},{13,15},{16,18},{17,... | collective-permute-start | bytes 589832 | tf_op jit(solution)/shard_map/ppermute | solution.py:741
  136.7 6.1 %collective-permute-start.16 = (bf16[2,24,2048]{2,1,0:T(8,128)(2,1)S(1)}, bf16[2,24,2048]{2,1,0:T(8,128)(2,1)S(1)}, u32[]{:S(2)}, u32[]{:S(2)}) collective-permute-start(bf16[2,24,2048]{2,1,0:T(8,128)(2,1)S(1)} %get-tuple-element.536), channel_id=1, source_target_pairs={{0,2},{1,3},{4,6},{5,7},{8,10},{9,11},{12,14},{13,15},{16,18},{17,... | collective-permute-start | bytes 589832 | tf_op jit(solution)/shard_map/ppermute | solution.py:741
  (2 other events, 4.2 us)
